TPU v7x, 128 devices: a whole 4x4x4 slice. The times are simulated.
128 devices in a mesh: dp: 2 (over core), fsdp: 64 (over z, y, x).
Axes of the slice: x: 4, y: 4, z: 4, core: 2. Of those that a mesh axis runs over, the one named last changes fastest.
Arguments:
- dec_in: bfloat16 [256, 512, 768], P(('dp', 'fsdp'))
- enc_out: bfloat16 [256, 768, 768], P(('dp', 'fsdp'))
- src_lens: int32 [256], P(('dp', 'fsdp'))
- tgt_lens: int32 [256], P(('dp', 'fsdp'))
- y_cot: bfloat16 [256, 512, 768], P(('dp', 'fsdp'))
- attn_w: bfloat16 [6144, 768], P('fsdp')
- ffn_w: bfloat16 [6144, 768], P('fsdp')
- vec_params: bfloat16 [14592], P('fsdp')
Outputs:
- output 1: bfloat16 [256, 512, 768], P(('dp', 'fsdp'))
- output 2: bfloat16 [256, 512, 768], P(('dp', 'fsdp'))
- output 3: bfloat16 [256, 768, 768], P(('dp', 'fsdp'))
- output 4: float32 [6144, 768], P('fsdp')
- output 5: float32 [6144, 768], P('fsdp')
- output 6: float32 [14592], P('fsdp')
All inputs are finite; a program needn't handle non-finite values.
Results may differ from a plain program's by a relative error of at most 0.016307.
Values are sent between devices in bfloat16 or wider.
A program may use at most 1 GiB of HBM per device.

v0:
```python
import functools
import jax
import jax.numpy as jnp
from jax import lax
from jax.experimental import pallas as pl
from jax.experimental.pallas import tpu as pltpu
from jax.sharding import PartitionSpec as P

ZERO, ONE, TWO, THREE = range(4)
ALL = ...
HEAD_DIM = 64
LN_EPS = 1e-5
MASK_FILL = -1e30
VMEM_BYTES = 60 * 1024 * 1024
F32 = jnp.float32
BF16 = jnp.bfloat16
GROUP = 256
PAIR = 128


SIDE = 4
LANES = 128
COLOURS = THREE
STAGES = TWO
DIM_ORDER = ((TWO, ONE, ZERO), (ONE, ZERO, TWO), (ZERO, TWO, ONE))
MESH_ID = pl.DeviceIdType.MESH


def torus_place():
    chip = lax.axis_index('fsdp')
    return (chip // (SIDE * SIDE), lax.rem(chip // SIDE, SIDE), lax.rem(chip, SIDE))


def chip_at(place, dim, shift):
    moved = [lax.rem(p + shift + SIDE, SIDE) if d == dim else p for d, p in enumerate(place)]
    return (moved[ZERO] * SIDE + moved[ONE]) * SIDE + moved[TWO]


def meet_neighbours(place):
    barrier = pltpu.get_barrier_semaphore()
    core = lax.axis_index('dp')
    for dim in range(THREE):
        for shift in (ONE, -ONE):
            pl.semaphore_signal(barrier, inc=ONE, device_id=(core, chip_at(place, dim, shift)), device_id_type=MESH_ID)
    pl.semaphore_signal(barrier, inc=ONE, device_id=(ONE - core, lax.axis_index('fsdp')), device_id_type=MESH_ID)
    pl.semaphore_wait(barrier, 7)


class Scatter:
    def __init__(self, scale, sources, outs, scratch, resident=False):
        self.scale, self.outs, self.resident = scale, outs, resident
        self.sources = [(ref, pl.ds(first, n)) for ref, first, n in sources]
        (self.acc, g1, d1, g2, d2, g3, d3, self.send_sem, self.recv_sem, self.load_sem, *stage) = scratch
        self.stage = None if resident else stage[ZERO]
        self.got, self.far = (g1, g2, g3), (d1, d2, d3)
        self.heights = [n for _, _, n in sources]
        self.offsets = [sum(self.heights[:i]) for i in range(len(sources))]
        self.height = sum(self.heights)
        self.n_low = self.heights[ZERO] // TWO
        self.core, self.chip, self.place = lax.axis_index('dp'), lax.axis_index('fsdp'), torus_place()
        self.pieces = [(d, colour) for d in (TWO, ONE, THREE, ZERO) for colour in range(COLOURS)]

    @staticmethod
    def scratch_shapes(heights, resident=False):
        h = sum(heights)
        n_low = heights[ZERO] // TWO
        buf = lambda *shape: pltpu.VMEM((COLOURS,) + shape + (LANES,), F32)
        n = Scatter.n_copies(len(heights))
        return [buf(SIDE, SIDE, SIDE, h), buf(TWO, SIDE, SIDE, h), buf(TWO, TWO, SIDE, h), buf(TWO, SIDE, h), buf(TWO, TWO, h), buf(TWO, h), buf(TWO, max(n_low, h - n_low)),
                pltpu.SemaphoreType.DMA((n,)), pltpu.SemaphoreType.DMA((n,)), pltpu.SemaphoreType.DMA((THREE + COLOURS, len(heights)))] + (
                    [] if resident else [pltpu.VMEM((STAGES, SIDE, SIDE, h, LANES), F32)])

    @staticmethod
    def n_copies(n_parts):
        return 12 * n_parts + COLOURS * 18 + COLOURS * n_parts

    def remote(self, i, src, dst, device):
        return pltpu.make_async_remote_copy(src_ref=src, dst_ref=dst, send_sem=self.send_sem.at[i], recv_sem=self.recv_sem.at[i], device_id=device, device_id_type=MESH_ID)

    def columns(self, of_core, colour):
        return pl.ds(pl.multiple_of((of_core * COLOURS + colour) * LANES, LANES), LANES)

    def slot(self, d, colour):
        dim = DIM_ORDER[colour][ZERO]
        where = [slice(None)] * THREE
        where[dim] = lax.rem(self.place[dim] + d, SIDE)
        return tuple(where)

    def rows_of(self, part):
        return pl.ds(self.offsets[part], self.heights[part])

    def swaps(self, piece):
        d, colour = self.pieces[piece]
        where, cols = self.slot(d, colour), self.columns(ONE - self.core, colour)
        n = len(self.sources)
        return [self.remote(piece * n + i, src.at[where + (rows, cols)], self.acc.at[(colour,) + where + (self.rows_of(i), slice(None))], (ONE - self.core, self.chip))
                for i, (src, rows) in enumerate(self.sources)]

    def loads(self, piece):
        d, colour = self.pieces[piece]
        where, cols = self.slot(d, colour), self.columns(self.core, colour)
        if self.resident:
            return []
        return [pltpu.make_async_copy(src.at[where + (rows, cols)], self.stage.at[piece % STAGES, :, :, self.rows_of(i), :], self.load_sem.at[piece % STAGES, i])
                for i, (src, rows) in enumerate(self.sources)]

    def split_rows(self, half):
        return pl.ds(ZERO, self.n_low) if half == ZERO else pl.ds(self.n_low, self.height - self.n_low)

    def block(self, colour, phase, d, half=None):
        order = DIM_ORDER[colour]
        where = [None, None, None]
        for done in order[:phase]:
            where[done] = self.place[done]
        where[order[phase]] = lax.rem(self.place[order[phase]] + d, SIDE)
        for i, rest in enumerate(sorted(order[phase + ONE:])):
            where[rest] = slice(None) if half is None or i > ZERO else pl.ds(TWO * half, TWO)
        rows = self.split_rows(half) if phase == TWO and half is not None else slice(None)
        return self.acc.at[(colour,) + tuple(where) + (rows, slice(None))]

    def got_half(self, colour, phase, direction, half):
        where = self.split_rows(half) if phase == TWO else pl.ds(TWO * half, TWO)
        return self.got[phase].at[colour, direction, where]

    def far_part(self, colour, phase, direction):
        if phase == TWO:
            return self.far[phase].at[colour, direction, pl.ds(ZERO, self.n_low if direction == ZERO else self.height - self.n_low), :]
        return self.far[phase].at[colour, direction]

    def ring(self, colour, phase, direction):
        shift = ONE - TWO * direction
        device = (self.core, chip_at(self.place, DIM_ORDER[colour][phase], shift))
        i = 12 * len(self.sources) + ((colour * THREE + phase) * TWO + direction) * THREE
        near = shift % SIDE
        return (self.remote(i, self.block(colour, phase, TWO, direction), self.far_part(colour, phase, direction), device),
                self.remote(i + ONE, self.block(colour, phase, near, ONE - direction), self.got_half(colour, phase, direction, ONE - direction), device),
                self.remote(i + TWO, self.block(colour, phase, near, direction), self.got_half(colour, phase, direction, direction), device))

    def gives(self, colour):
        n = len(self.sources)
        base = 12 * n + COLOURS * 18 + colour * n
        done = self.acc.at[colour, self.place[ZERO], self.place[ONE], self.place[TWO]]
        cols = self.columns(self.core, colour)
        pairs = [(done.at[self.rows_of(i), :], out.at[:, cols]) for i, out in enumerate(self.outs)]
        return [(self.remote(base + i, src, dst, (ONE - self.core, self.chip)), pltpu.make_async_copy(src, dst, self.load_sem.at[THREE + colour, i])) for i, (src, dst) in enumerate(pairs)]

    def add_into(self, dst, sources, n_lead):
        def body(i, _):
            total = dst[i]
            for src in sources:
                total = total + src[i]
            dst[i] = total
            return ZERO

        if n_lead == TWO:
            lax.fori_loop(ZERO, dst.shape[ZERO], body, ZERO)
        else:
            total = dst[ALL]
            for src in sources:
                total = total + src[ALL]
            dst[ALL] = total


    def begin(self):
        for piece in range(STAGES):
            for copy in self.loads(piece):
                copy.start()
        for piece in range(len(self.pieces)):
            for copy in self.swaps(piece):
                copy.start()

    def absorb(self, turn):
        for piece in range(turn * COLOURS, (turn + ONE) * COLOURS):
            d, colour = self.pieces[piece]
            for copy in self.loads(piece):
                copy.wait()
            for copy in self.swaps(piece):
                copy.wait_recv()
            where = self.slot(d, colour)
            if self.resident:
                for i, (src, rows) in enumerate(self.sources):
                    self.add_into(self.acc.at[(colour,) + where + (self.rows_of(i), slice(None))], [src.at[where + (rows, self.columns(self.core, colour))]], TWO)
            else:
                self.add_into(self.acc.at[(colour,) + where], [self.stage.at[piece % STAGES]], TWO)
            if piece + STAGES < len(self.pieces):
                for copy in self.loads(piece + STAGES):
                    copy.start()
            if turn == ZERO:
                for direction in range(TWO):
                    self.ring(colour, ZERO, direction)[ZERO].start()
            elif turn < THREE:
                self.ring(colour, ZERO, turn - ONE)[ONE].start()

    def relay(self, phase):
        for colour in range(COLOURS):
            for direction in range(TWO):
                far, _, fed = self.ring(colour, phase, direction)
                far.wait_recv()
                self.add_into(self.block(colour, phase, (ONE - TWO * direction) % SIDE, direction), [self.far_part(colour, phase, direction)], TWO - phase)
            for direction in range(TWO):
                self.ring(colour, phase, direction)[TWO].start()

    def settle(self, phase):
        for colour in range(COLOURS):
            for direction in range(TWO):
                _, own, fed = self.ring(colour, phase, direction)
                own.wait_recv()
                fed.wait_recv()
            self.add_into(self.block(colour, phase, ZERO), [self.got[phase].at[colour, direction] for direction in range(TWO)], TWO - phase)
            if phase < TWO:
                for kind in range(TWO):
                    for direction in range(TWO):
                        self.ring(colour, phase + ONE, direction)[kind].start()
            else:
                done = self.acc.at[colour, self.place[ZERO], self.place[ONE], self.place[TWO]]
                done[ALL] = done[ALL] * self.scale
                for give, keep in self.gives(colour):
                    keep.start()
                    give.start()

    def end(self):
        for colour in range(COLOURS):
            for give, keep in self.gives(colour):
                give.wait_recv()
                give.wait_send()
                keep.wait()
        for piece in range(len(self.pieces)):
            for copy in self.swaps(piece):
                copy.wait_send()
        for colour in range(COLOURS):
            for phase in range(THREE):
                for direction in range(TWO):
                    for copy in self.ring(colour, phase, direction):
                        copy.wait_send()


def rs_kernel(scale, *refs):
    scatter = Scatter(scale, [(ref, ZERO, ref.shape[THREE]) for ref in refs[:TWO]], refs[TWO:4], refs[4:])
    meet_neighbours(scatter.place)
    scatter.begin()
    for turn in range(THREE):
        scatter.absorb(turn)
    scatter.relay(ZERO)
    scatter.absorb(THREE)
    scatter.settle(ZERO)
    for phase in (ONE, TWO):
        scatter.relay(phase)
        scatter.settle(phase)
    scatter.end()


def as_torus(rows):
    return rows.reshape(SIDE, SIDE, SIDE, rows.shape[ZERO] // SIDE ** THREE, rows.shape[ONE])


def scatter_grads(g_attn, g_vec, scale):
    sources = [as_torus(g_attn), as_torus(g_vec)]
    heights = [src.shape[THREE] for src in sources]
    width = g_attn.shape[ONE]
    anywhere = pl.BlockSpec(memory_space=pl.ANY)
    return pl.pallas_call(
        functools.partial(rs_kernel, scale),
        in_specs=[anywhere] * TWO, out_specs=[anywhere] * TWO,
        out_shape=[jax.ShapeDtypeStruct((h, width), F32) for h in heights],
        scratch_shapes=Scatter.scratch_shapes(heights),
        compiler_params=pltpu.CompilerParams(collective_id=ONE, has_side_effects=True, vmem_limit_bytes=VMEM_BYTES),
        cost_estimate=pl.CostEstimate(flops=10 ** 9, bytes_accessed=8 * width * g_attn.shape[ZERO], transcendentals=ZERO),
        name='scatter_grads',
    )(*sources)


class Gather:
    def __init__(self, send_sem, recv_sem, base=ZERO):
        self.send_sem, self.recv_sem = send_sem, recv_sem
        self.used = base
        self.core, self.chip, self.place = lax.axis_index('dp'), lax.axis_index('fsdp'), torus_place()
        self.sibling = (ONE - self.core, self.chip)
        self.started = []

    def remote(self, src, dst, device):
        i = self.used
        self.used += ONE
        return pltpu.make_async_remote_copy(src_ref=src, dst_ref=dst, send_sem=self.send_sem.at[i], recv_sem=self.recv_sem.at[i], device_id=device, device_id_type=MESH_ID)

    def start(self, copy):
        copy.start()
        self.started.append(copy)

    def ring(self, colour, phase, view, own=None, split=False):
        order = DIM_ORDER[colour]
        dim = order[phase]
        have = sorted(order[:phase])

        def index(shift, half=None):
            where = [self.place[ZERO], self.place[ONE], self.place[TWO]]
            where[dim] = lax.rem(self.place[dim] + shift + SIDE, SIDE)
            for i, h in enumerate(have):
                where[h] = slice(None) if half is None or i > ZERO else pl.ds(TWO * half, TWO)
            return tuple(where)

        out = []
        for direction, shift in enumerate((ONE, -ONE)):
            device = (self.core, chip_at(self.place, dim, shift))
            half = direction if phase == ZERO else None
            near_dst = view(index(ZERO), None)
            if split:
                near = [self.remote(view(index(ZERO, h), None), view(index(ZERO, h), None), device) for h in (direction, ONE - direction)]
            else:
                near = [self.remote(near_dst if own is None else own, near_dst, device)]
            out.append(dict(
                near=near,
                far=self.remote(view(index(-shift, direction), half), view(index(-shift, direction), half), device),
                near_at=index(-shift), far_at=index(TWO, direction)))
        return out


def ag_kernel(attn_ref, ffn_ref, vec_ref, oattn_ref, planes_ref, vec_out, attn_v, send_sem, recv_sem, load_sem):
    net = Gather(send_sem, recv_sem)
    core, place = net.core, net.place
    rows, width = attn_ref.shape
    band = rows // (TWO * COLOURS)
    vec_high = vec_ref.shape[ZERO]
    stores, finals = [], []

    def band_rows(colour):
        return pl.ds(pl.multiple_of((core * COLOURS + colour) * band, band), band)

    def columns(half):
        return slice(None) if half is None else pl.ds(half * (width // TWO), width // TWO)

    def attn_view(colour):
        return lambda where, half: attn_v.at[where + (band_rows(colour), columns(half))]

    def ffn_view(colour):
        last = DIM_ORDER[colour][TWO]
        return lambda where, half: planes_ref.at[(colour,) + tuple(w for d, w in enumerate(where) if d != last) + (slice(None), columns(half))]

    def vec_view(where, half):
        return vec_out.at[where + (slice(None) if half is None else pl.ds(half * (vec_high // TWO), vec_high // TWO), slice(None))]

    colours = range(COLOURS)
    attn_own = [attn_ref.at[band_rows(colour), :] for colour in colours]
    ffn_own = [ffn_ref.at[band_rows(colour), :] for colour in colours]
    rings = {('attn', phase): [net.ring(colour, phase, attn_view(colour), attn_own[colour] if phase == ZERO else None, phase > ZERO) for colour in colours] for phase in range(THREE)}
    rings |= {('ffn', phase): [net.ring(colour, phase, ffn_view(colour), ffn_own[colour] if phase == ZERO else None, phase > ZERO) for colour in colours] for phase in range(TWO)}
    rings |= {('vec', phase): [net.ring(ONE, phase, vec_view, vec_ref if phase == ZERO else None)] for phase in range(THREE)}

    def publish(at):
        keep = pltpu.make_async_copy(attn_v.at[at], oattn_ref.at[at], load_sem.at[len(stores)])
        keep.start()
        stores.append(keep)
        give = net.remote(attn_v.at[at], oattn_ref.at[at], net.sibling)
        net.start(give)
        finals.append(give)

    def send_near(name, phase):
        for ring in rings.get((name, phase), ()):
            for way in ring:
                for copy in way['near']:
                    net.start(copy)

    def pass_on(name, phase):
        for ring in rings.get((name, phase), ()):
            for way in ring:
                way['near'][ZERO].wait_recv()
                net.start(way['far'])
        if phase == TWO and name == 'attn':
            for colour in colours:
                for way in rings[(name, phase)][colour]:
                    way['near'][ONE].wait_recv()
                    publish(way['near_at'] + (band_rows(colour), slice(None)))

    def complete(name, phase):
        for colour, ring in enumerate(rings.get((name, phase), ())):
            for way in ring:
                way['far'].wait_recv()
                if phase == ONE and name != 'vec':
                    way['near'][ONE].wait_recv()
            if phase < TWO and (name, phase + ONE) in rings:
                for way in rings[(name, phase + ONE)][colour]:
                    for copy in way['near']:
                        net.start(copy)
            if phase == TWO and name == 'attn':
                for way in ring:
                    publish(way['far_at'] + (band_rows(colour), slice(None)))
        if phase == ONE and name == 'attn':
            for colour in colours:
                last = DIM_ORDER[colour][TWO]
                publish(tuple(place[d] if d == last else slice(None) for d in range(THREE)) + (band_rows(colour), slice(None)))

    for colour in colours:
        attn_v[(place[ZERO], place[ONE], place[TWO]) + (band_rows(colour), slice(None))] = attn_ref[band_rows(colour), :]
        kept = [place[d] for d in range(THREE) if d != DIM_ORDER[colour][TWO]]
        planes_ref[(colour, kept[ZERO], kept[ONE])] = ffn_ref[band_rows(colour), :]
    vec_out[place[ZERO], place[ONE], place[TWO]] = vec_ref[ALL]
    meet_neighbours(place)
    names = ('attn', 'vec', 'ffn')
    for name in names:
        send_near(name, ZERO)
    for phase in range(THREE):
        for name in names:
            pass_on(name, phase)
        for name in names:
            complete(name, phase)
    for copy in finals:
        copy.wait_recv()
    for copy in net.started:
        copy.wait_send()
    for copy in stores:
        copy.wait()


def gather_params(attn_w, ffn_w, vec_rows):
    rows, width = attn_w.shape
    full = (SIDE, SIDE, SIDE, rows, width)
    n_copies = COLOURS * (4 * TWO + 6 * THREE) + 4 * THREE + COLOURS * 5
    vmem = pl.BlockSpec(memory_space=pltpu.VMEM)
    return pl.pallas_call(
        ag_kernel,
        in_specs=[vmem] * THREE, out_specs=[pl.BlockSpec(memory_space=pl.ANY), vmem, vmem],
        out_shape=[jax.ShapeDtypeStruct(full, BF16), jax.ShapeDtypeStruct((COLOURS, SIDE, SIDE, rows // (TWO * COLOURS), width), BF16),
                   jax.ShapeDtypeStruct((SIDE, SIDE, SIDE) + vec_rows.shape, F32)],
        scratch_shapes=[pltpu.VMEM(full, BF16), pltpu.SemaphoreType.DMA((n_copies,)), pltpu.SemaphoreType.DMA((n_copies,)), pltpu.SemaphoreType.DMA((COLOURS * 5,))],
        compiler_params=pltpu.CompilerParams(collective_id=TWO, has_side_effects=True, vmem_limit_bytes=VMEM_BYTES),
        cost_estimate=pl.CostEstimate(flops=10 ** 9, bytes_accessed=4 * rows * width * SIDE ** THREE, transcendentals=ZERO),
        name='gather_params',
    )(attn_w, ffn_w, vec_rows)


class LastPhase:
    def __init__(self, planes, out, near, far, send_sem, recv_sem, load_sem):
        self.planes, self.out, self.near, self.far = planes, out, near, far
        self.send_sem, self.recv_sem, self.load_sem = send_sem, recv_sem, load_sem
        self.core, self.chip, self.place = lax.axis_index('dp'), lax.axis_index('fsdp'), torus_place()
        self.band = planes.shape[THREE]

    @staticmethod
    def scratch_shapes(planes):
        colours, side, _, band, width = planes.shape
        sems = [pltpu.SemaphoreType.DMA((11 * COLOURS,)), pltpu.SemaphoreType.DMA((11 * COLOURS,)), pltpu.SemaphoreType.DMA((5 * COLOURS,))]
        return [pltpu.VMEM((colours, TWO, side, side, band, width), BF16), pltpu.VMEM((colours, TWO, side // TWO, side, band, width), BF16)] + sems

    def remote(self, i, src, dst, device):
        return pltpu.make_async_remote_copy(src_ref=src, dst_ref=dst, send_sem=self.send_sem.at[i], recv_sem=self.recv_sem.at[i], device_id=device, device_id_type=MESH_ID)

    def ring(self, colour, direction):
        device = (self.core, chip_at(self.place, DIM_ORDER[colour][TWO], ONE - TWO * direction))
        i = 11 * colour + THREE * direction
        got = self.near.at[colour, direction]
        near = [self.remote(i + n, self.planes.at[colour, pl.ds(TWO * half, TWO)], got.at[pl.ds(TWO * half, TWO)], device) for n, half in enumerate((direction, ONE - direction))]
        return near + [self.remote(i + TWO, got.at[pl.ds(TWO * direction, TWO)], self.far.at[colour, direction], device)]

    def shares(self, colour):
        last = DIM_ORDER[colour][TWO]
        rows = pl.ds(pl.multiple_of((self.core * COLOURS + colour) * self.band, self.band), self.band)
        views = [(self.planes.at[colour], ZERO, None)]
        views += [(self.near.at[colour, direction], TWO * direction - ONE, None) for direction in range(TWO)]
        views += [(self.far.at[colour, direction], TWO, direction) for direction in range(TWO)]
        out = []
        for n, (src, shift, half) in enumerate(views):
            where = [slice(None)] * THREE
            where[last] = lax.rem(self.place[last] + shift + SIDE, SIDE)
            if half is not None:
                where[min(d for d in range(THREE) if d != last)] = pl.ds(TWO * half, TWO)
            dst = self.out.at[tuple(where) + (rows, slice(None))]
            out.append((self.remote(11 * colour + 6 + n, src, dst, (ONE - self.core, self.chip)), pltpu.make_async_copy(src, dst, self.load_sem.at[5 * colour + n])))
        return out

    def share(self, colour, which):
        for n in which:
            give, keep = self.shares(colour)[n]
            give.start()
            keep.start()

    def begin(self):
        for colour in range(COLOURS):
            for direction in range(TWO):
                for copy in self.ring(colour, direction)[:TWO]:
                    copy.start()
        for colour in range(COLOURS):
            self.share(colour, (ZERO,))

    def pass_on(self):
        for colour in range(COLOURS):
            for direction in range(TWO):
                first, _, far = self.ring(colour, direction)
                first.wait_recv()
                far.start()
        for colour in range(COLOURS):
            for direction in range(TWO):
                self.ring(colour, direction)[ONE].wait_recv()
            self.share(colour, (ONE, TWO))

    def complete(self):
        for colour in range(COLOURS):
            for direction in range(TWO):
                self.ring(colour, direction)[TWO].wait_recv()
            self.share(colour, (THREE, 4))

    def end(self):
        for colour in range(COLOURS):
            for give, keep in self.shares(colour):
                give.wait_recv()
                give.wait_send()
                keep.wait()
            for direction in range(TWO):
                for copy in self.ring(colour, direction):
                    copy.wait_send()


def dot(lhs, rhs, contract=((ONE,), (ZERO,))):
    return lax.dot_general(lhs, rhs, (contract, ((), ())), preferred_element_type=F32)


def dot_nt(lhs, rhs):
    return dot(lhs, rhs, ((ONE,), (ONE,)))


def dot_tn(lhs, rhs):
    return dot(lhs, rhs, ((ZERO,), (ZERO,)))


def norm_rows(resid, gain, shift):
    mean = jnp.mean(resid, axis=-ONE, keepdims=True)
    centred = resid - mean
    inv_std = lax.rsqrt(jnp.mean(centred * centred, axis=-ONE, keepdims=True) + LN_EPS)
    normed = centred * inv_std
    return (normed * gain + shift).astype(BF16), normed, inv_std


def norm_rows_bwd(d_out, normed, inv_std, gain):
    d_norm = d_out * gain
    return inv_std * (d_norm - jnp.mean(d_norm, axis=-ONE, keepdims=True) - normed * jnp.mean(d_norm * normed, axis=-ONE, keepdims=True))


def col_sum(values):
    return jnp.sum(values, axis=ZERO, keepdims=True)


def lane_row(head, dtype=BF16):
    lane = lax.broadcasted_iota(jnp.int32, (ONE, PAIR), ONE)
    return jnp.where((lane >= HEAD_DIM * head) & (lane < HEAD_DIM * (head + ONE)), 1.0, 0.0).astype(dtype)


def spare_lane(head):
    lane = lax.broadcasted_iota(jnp.int32, (ONE, PAIR), ONE)
    return jnp.where(lane == HEAD_DIM * (ONE - head), 1.0, 0.0)


def mask_fill(n_rows, n_valid):
    row = lax.broadcasted_iota(jnp.int32, (n_rows, PAIR), ZERO)
    return jnp.where(row >= n_valid, MASK_FILL, 0.0)


def head_masks(pair_q, pair_k, head, fill):
    q_f = pair_q * lane_row(head) + spare_lane(head).astype(BF16)
    k_f = pair_k * lane_row(head) + (fill * spare_lane(head)).astype(BF16)
    return q_f, k_f


def half_only(pair, head):
    return pair * lane_row(head)


def join_halves(first, second):
    lane = lax.broadcasted_iota(jnp.int32, first.shape, ONE)
    return jnp.where(lane < HEAD_DIM, first, second)


def score_blocks(n_heads, n_q, n_k, causal, step):
    if not causal:
        return [(head, ZERO, n_q, n_k) for head in range(n_heads)]
    return [(head, first, step, first + step) for head in range(n_heads) for first in range(ZERO, n_q, step)]


def scores_t(q_f, k_f, causal, first):
    s_t = dot_nt(k_f, q_f)
    if causal:
        key_i = lax.broadcasted_iota(jnp.int32, s_t.shape, ZERO)
        qry_i = lax.broadcasted_iota(jnp.int32, s_t.shape, ONE) + first
        s_t = jnp.where(key_i <= qry_i, s_t, MASK_FILL)
    return s_t


def pair_of(group, head):
    return group[:, head // TWO * PAIR:(head // TWO + ONE) * PAIR]


def masked_pairs(q_g, k_g, n_valid):
    fill = mask_fill(k_g.shape[ZERO], n_valid)
    cache = {}

    def get(head):
        if head not in cache:
            cache[head] = head_masks(pair_of(q_g, head), pair_of(k_g, head), head % TWO, fill)
        return cache[head]

    return get


def stack_heads(parts, n_heads):
    return jnp.concatenate([jnp.concatenate(parts[head], axis=ONE) for head in range(n_heads)], axis=ZERO)


def run_ahead(blocks, produce, transform, consume, delay):
    ahead = produce(blocks[ZERO])
    waiting = []
    for i, block in enumerate(blocks):
        now = ahead
        if i + ONE < len(blocks):
            ahead = produce(blocks[i + ONE])
        waiting.append((block, transform(block, now)))
        if len(waiting) > delay:
            consume(*waiting.pop(ZERO))
    for item in waiting:
        consume(*item)


def attend_group(q_g, k_g, v_g, n_valid, causal, lse_ref):
    n_heads = GROUP // HEAD_DIM
    o_parts = [[] for _ in range(n_heads)]
    v_t = v_g.T
    masked = masked_pairs(q_g, k_g, n_valid)

    def produce(block):
        head, first, n_q, n_k = block
        q_f, k_f = masked(head)
        return scores_t(q_f[first:first + n_q], k_f[:n_k], causal, first)

    def transform(block, s_t):
        head, first, n_q, n_k = block
        top = jnp.max(s_t, axis=ZERO, keepdims=True)
        e_t = jnp.exp(s_t - top)
        total = jnp.sum(e_t, axis=ZERO, keepdims=True)
        lse_ref[ZERO, ZERO, head // TWO, head % TWO:head % TWO + ONE, first:first + n_q] = top + jnp.log(total)
        return (e_t * (1.0 / total)).astype(BF16)

    def consume(block, p_t):
        head, first, n_q, n_k = block
        o_parts[head].append(dot(v_t[HEAD_DIM * head:HEAD_DIM * (head + ONE), :n_k], p_t))

    run_ahead(score_blocks(n_heads, q_g.shape[ZERO], k_g.shape[ZERO], causal, 128), produce, transform, consume, TWO)
    return stack_heads(o_parts, n_heads).T.astype(BF16)


def attend_group_bwd(d_o, q_g, k_g, v_g, n_valid, causal, lse_ref):
    n_heads = q_g.shape[ONE] // HEAD_DIM
    k_t = k_g.T
    dq_t, dk_h, dv_h = [[] for _ in range(n_heads)], [None] * n_heads, [None] * n_heads
    masked = masked_pairs(q_g, k_g, n_valid)
    v_half = {}

    def produce(block):
        head, first, n_q, n_k = block
        q_f, k_f = masked(head)
        if head not in v_half:
            v_half[head] = half_only(pair_of(v_g, head), head % TWO)
        rows = slice(first, first + n_q)
        return scores_t(q_f[rows], k_f[:n_k], causal, first), dot_nt(v_half[head][:n_k], pair_of(d_o, head)[rows])

    def transform(block, products):
        head, first, n_q, n_k = block
        s_t, dp_t = products
        p_t = jnp.exp(s_t - lse_ref[head // TWO, head % TWO:head % TWO + ONE, first:first + n_q])
        weighted = p_t * dp_t
        return p_t.astype(BF16), (weighted - p_t * jnp.sum(weighted, axis=ZERO, keepdims=True)).astype(BF16)

    def grow(old, new):
        if old is None:
            return new
        n_old = old.shape[ZERO]
        return old + new if n_old == new.shape[ZERO] else jnp.concatenate([old + new[:n_old], new[n_old:]], axis=ZERO)

    def consume(block, operands):
        head, first, n_q, n_k = block
        p_b, ds_t = operands
        rows = slice(first, first + n_q)
        dv_h[head] = grow(dv_h[head], dot(p_b, pair_of(d_o, head)[rows]))
        dk_h[head] = grow(dk_h[head], dot(ds_t, pair_of(q_g, head)[rows]))
        dq_t[head].append(dot(k_t[HEAD_DIM * head:HEAD_DIM * (head + ONE), :n_k], ds_t))

    run_ahead(score_blocks(n_heads, q_g.shape[ZERO], k_g.shape[ZERO], causal, 256), produce, transform, consume, ZERO)
    join = lambda parts: jnp.concatenate([join_halves(parts[h], parts[h + ONE]) for h in range(ZERO, n_heads, TWO)], axis=ONE)
    return stack_heads(dq_t, n_heads).T * 0.125, join(dk_h), join(dv_h)


def attn_fwd_kernel(causal, slots, guest, lens_ref, x_ref, kv_ref, wq_ref, wk_ref, wv_ref, w_all, bias_ref, rows_ref,
                    q_ref, k_ref, v_ref, o_ref, lse_ref, h_ref, normed_ref, inv_ref, o_all, wo_v, load_sem):
    q_row, k_row, v_row, o_row, gain_row, o_mat = slots
    sample, group = pl.program_id(ZERO), pl.program_id(ONE)
    d_model = wo_v.shape[ZERO]
    fetch = pltpu.make_async_copy(w_all.at[pl.ds(o_mat * d_model, d_model), :], wo_v, load_sem)

    @pl.when((sample == ZERO) & (group == ZERO))
    def _():
        fetch.start()

    turn = sample * pl.num_programs(ONE) + group
    if guest is not None:
        for where, steps in ((ZERO, (lambda: meet_neighbours(guest.place), guest.begin)), (THREE, (guest.pass_on,)), (5, (guest.complete,))):
            @pl.when(turn == where)
            def _():
                for step in steps:
                    step()

    x_b, kv_b = x_ref[ALL], kv_ref[ALL]
    q_g = ((dot(x_b, wq_ref[ALL]) + bias_ref[q_row:q_row + ONE, :]) * 0.125).astype(BF16)
    k_g = (dot(kv_b, wk_ref[ALL]) + bias_ref[k_row:k_row + ONE, :]).astype(BF16)
    v_g = (dot(kv_b, wv_ref[ALL]) + bias_ref[v_row:v_row + ONE, :]).astype(BF16)
    q_ref[ALL], k_ref[ALL], v_ref[ALL] = q_g, k_g, v_g
    o_g = attend_group(q_g, k_g, v_g, lens_ref[sample], causal, lse_ref)
    o_ref[ALL] = o_g
    o_all[:, pl.ds(pl.multiple_of(group * GROUP, GROUP), GROUP)] = o_g

    @pl.when((sample == ZERO) & (group == pl.num_programs(ONE) - ONE))
    def _():
        fetch.wait()

    @pl.when(group == pl.num_programs(ONE) - ONE)
    def _():
        resid = x_ref[ALL].astype(F32) + dot(o_all[ALL], wo_v[ALL]) + rows_ref[o_row:o_row + ONE, :]
        h_out, normed, inv_std = norm_rows(resid, rows_ref[gain_row:gain_row + ONE, :], rows_ref[gain_row + ONE:gain_row + TWO, :])
        h_ref[ALL], normed_ref[ALL], inv_ref[ALL] = h_out, normed, inv_std

    if guest is not None:
        @pl.when(turn == pl.num_programs(ZERO) * pl.num_programs(ONE) - ONE)
        def _():
            guest.end()


def attn_forward(x, kv, lens, attn_full, bias_rows, mats, slots, causal, planes=None, full_rows=None):
    d_model = x.shape[-ONE]
    n_batch = lens.shape[ZERO]
    n_q, n_k = x.shape[ZERO] // n_batch, kv.shape[ZERO] // n_batch
    n_groups = d_model // GROUP
    col = lambda mat: pl.BlockSpec((d_model, GROUP), lambda b, g: (mat, g))
    q_blk = pl.BlockSpec((n_q, GROUP), lambda b, g: (b, g))
    k_blk = pl.BlockSpec((n_k, GROUP), lambda b, g: (b, g))
    tok = lambda n: pl.BlockSpec((n, d_model), lambda b, g: (b, ZERO))
    n_heads_g = GROUP // HEAD_DIM
    out_shape = (
        jax.ShapeDtypeStruct(x.shape, BF16), jax.ShapeDtypeStruct(kv.shape, BF16), jax.ShapeDtypeStruct(kv.shape, BF16),
        jax.ShapeDtypeStruct(x.shape, BF16), jax.ShapeDtypeStruct((n_batch, n_groups, n_heads_g // TWO, TWO, n_q), F32),
        jax.ShapeDtypeStruct(x.shape, BF16), jax.ShapeDtypeStruct(x.shape, F32), jax.ShapeDtypeStruct((x.shape[ZERO], ONE), F32))
    kernel = functools.partial(attn_fwd_kernel, causal, slots + (mats[THREE],))
    in_specs = [pl.BlockSpec(memory_space=pltpu.SMEM), tok(n_q), tok(n_k), col(mats[ZERO]), col(mats[ONE]), col(mats[TWO]), pl.BlockSpec(memory_space=pl.ANY),
                pl.BlockSpec((bias_rows.shape[ZERO], GROUP), lambda b, g: (ZERO, g)), pl.BlockSpec(bias_rows.shape, lambda b, g: (ZERO, ZERO))]
    out_specs = [q_blk, k_blk, k_blk, q_blk, pl.BlockSpec((ONE, ONE, n_heads_g // TWO, TWO, n_q), lambda b, g: (b, g, ZERO, ZERO, ZERO)),
                 tok(n_q), tok(n_q), pl.BlockSpec((n_q, ONE), lambda b, g: (b, ZERO))]
    scratch = [pltpu.VMEM((n_q, d_model), BF16), pltpu.VMEM((d_model, d_model), BF16), pltpu.SemaphoreType.DMA]
    args = [lens, x, kv, attn_full, attn_full, attn_full, attn_full, bias_rows, bias_rows]
    params = dict(vmem_limit_bytes=VMEM_BYTES, dimension_semantics=('arbitrary', 'arbitrary'))
    if planes is None:
        body = functools.partial(kernel, None)
    else:
        n_in, n_out, n_own = len(args), len(out_specs), len(scratch)

        def body(*refs):
            ins, held, outs, whole, rest = refs[:n_in], refs[n_in], refs[n_in + ONE:n_in + ONE + n_out], refs[n_in + ONE + n_out], refs[n_in + TWO + n_out:]
            kernel(LastPhase(held, whole, *rest[n_own:]), *ins, *outs, *rest[:n_own])

        in_specs.append(pl.BlockSpec(memory_space=pltpu.VMEM))
        args.append(planes)
        out_specs.append(pl.BlockSpec(memory_space=pl.ANY))
        out_shape += (jax.ShapeDtypeStruct((SIDE, SIDE, SIDE, full_rows // SIDE ** THREE, d_model), BF16),)
        scratch += LastPhase.scratch_shapes(planes)
        params |= dict(collective_id=5, has_side_effects=True)
    return pl.pallas_call(
        body, grid=(n_batch, n_groups), in_specs=in_specs, out_specs=out_specs, out_shape=out_shape, scratch_shapes=scratch,
        compiler_params=pltpu.CompilerParams(**params),
        cost_estimate=pl.CostEstimate(flops=TWO * d_model * d_model * (TWO * x.shape[ZERO] + TWO * kv.shape[ZERO]) + 16 * x.shape[ZERO] * n_k * d_model, bytes_accessed=20 * x.shape[ZERO] * d_model, transcendentals=ZERO),
        name='attn_fwd',
    )(*args)


def attn_bwd_kernel(causal, gain_row, mats, guest, lens_ref, dres_ref, wo_ref, w_all, q_ref, k_ref, v_ref, lse_ref,
                    rows_ref, normed_ref, inv_ref, lhs_refs, dx_ref, dkv_ref, sums_ref, tail_ref, grads_ref,
                    rhs_q, rhs_k, lhs_q, lhs_k, do_v, w_v, grad_v, load_sem, store_sem):
    sample, group = pl.program_id(ZERO), pl.program_id(ONE)
    d_model = w_v.shape[ONE]
    n_q, n_k = q_ref.shape[ZERO], k_ref.shape[ZERO]
    last = pl.num_programs(ONE) - ONE
    fetches = [pltpu.make_async_copy(w_all.at[pl.ds(mat * d_model, d_model), :], w_v.at[i], load_sem.at[i]) for i, mat in enumerate(mats[:THREE])]
    dk_all, dv_all = (rhs_q.at[ONE], rhs_q.at[TWO]) if causal else (rhs_k.at[ZERO], rhs_k.at[ONE])
    d_all, dres_all = rhs_q.at[ZERO], rhs_q.at[THREE if causal else ONE]
    places = (lhs_q.at[ZERO], lhs_q.at[ONE]) if causal else (lhs_q.at[ZERO], lhs_k, lhs_q.at[ZERO])
    lhs_fetch = lambda i: pltpu.make_async_copy(lhs_refs[i], places[i], load_sem.at[THREE + i])
    store = lambda buf, mat: pltpu.make_async_copy(grad_v.at[buf], grads_ref.at[pl.ds(pl.multiple_of(mat * d_model, d_model), d_model), :], store_sem.at[buf])

    @pl.when((sample == ZERO) & (group == ZERO))
    def _():
        for fetch in fetches + [lhs_fetch(ZERO), lhs_fetch(ONE)]:
            fetch.start()

    turn = sample * pl.num_programs(ONE) + group
    q_rows = pl.ds(pl.multiple_of(sample * n_q, n_q), n_q)
    k_rows = pl.ds(pl.multiple_of(sample * n_k, n_k), n_k)
    d_o = dot_nt(dres_ref[ALL].astype(BF16), wo_ref[ALL]).astype(BF16)

    def keep(found, first, width):
        here = pl.ds(first, width)
        cols = pl.ds(pl.multiple_of(group * GROUP + first, PAIR), width)
        for i, (full, rows, value) in enumerate(zip((d_all, dk_all, dv_all), (q_rows, k_rows, k_rows), found)):
            sums_ref[ZERO, i:i + ONE, here] = col_sum(value)
            full[rows, cols] = value.astype(BF16)

    if causal:
        keep(attend_group_bwd(d_o, q_ref[ALL], k_ref[ALL], v_ref[ALL], lens_ref[sample], causal, lse_ref.at[ZERO, ZERO]), ZERO, GROUP)
    else:
        do_v[ALL] = d_o

        def one_pair(pair, _):
            guest(ZERO, TWO * turn + pair)
            first = pl.multiple_of(pair * PAIR, PAIR)
            here = pl.ds(first, PAIR)
            keep(attend_group_bwd(do_v[:, here], q_ref[:, here], k_ref[:, here], v_ref[:, here], lens_ref[sample], causal, lse_ref.at[ZERO, ZERO, pl.ds(pair, ONE)]), first, PAIR)
            return ZERO

        lax.fori_loop(ZERO, GROUP // PAIR, one_pair, ZERO)

    @pl.when(group == ZERO)
    def _():
        dres_all[q_rows, :] = dres_ref[ALL].astype(BF16)

    @pl.when((sample == ZERO) & (group == last))
    def _():
        for fetch in fetches:
            fetch.wait()

    guest(THREE, turn)

    @pl.when(group == last)
    def _():
        d_kv = dot_nt(dk_all[k_rows, :], w_v[ONE]) + dot_nt(dv_all[k_rows, :], w_v[TWO])
        d_h = dres_ref[ALL] + dot_nt(d_all[q_rows, :], w_v[ZERO])
        if causal:
            dx_ref[ALL] = (d_h + d_kv).astype(BF16)
            tail_ref[ALL] = jnp.zeros_like(tail_ref)
        else:
            dkv_ref[ALL] = d_kv.astype(BF16)
            normed = normed_ref[ALL]
            d_resid = norm_rows_bwd(d_h, normed, inv_ref[ALL], rows_ref[gain_row:gain_row + ONE, :])
            dx_ref[ALL] = d_resid
            tail_ref[ZERO, ZERO:ONE, :] = col_sum(d_resid)
            tail_ref[ZERO, ONE:TWO, :] = col_sum(d_h * normed)
            tail_ref[ZERO, TWO:THREE, :] = col_sum(d_h)

    @pl.when(turn == pl.num_programs(ZERO) * pl.num_programs(ONE) - ONE)
    def _():
        guest(TWO, 12)
        lhs_fetch(ZERO).wait()
        if causal:
            lhs_fetch(ONE).wait()

            def square(i, _):
                @pl.when(i >= TWO)
                def _():
                    store(i % TWO, mats[ZERO]).wait()

                grad_v[i % TWO] = dot_tn(lhs_q[i // THREE], rhs_q[i])
                store(i % TWO, mats[ZERO] + i).start()
                return ZERO

            lax.fori_loop(ZERO, 4, square, ZERO)
        else:
            def square_q(i, _):
                @pl.when(i == ONE)
                def _():
                    lhs_fetch(TWO).start()
                    lhs_fetch(TWO).wait()

                grad_v[i] = dot_tn(lhs_q[ZERO], rhs_q[i])
                store(i, mats[ZERO] + THREE * i).start()
                return ZERO

            def square_k(i, _):
                store(i, mats[ONE]).wait()
                grad_v[i] = dot_tn(lhs_k[ALL], rhs_k[i])
                store(i, mats[ONE] + i).start()
                return ZERO

            lax.fori_loop(ZERO, TWO, square_q, ZERO)
            guest(TWO, 13)
            lhs_fetch(ONE).wait()
            lax.fori_loop(ZERO, TWO, square_k, ZERO)
            guest(TWO, 14)
        for buf in range(TWO):
            store(buf, mats[ZERO]).wait()


def scatter_guest(scatter, plan, parity, position):
    steps = dict(end=scatter.end) | {('relay', p): functools.partial(scatter.relay, p) for p in range(THREE)}
    steps |= {('settle', p): functools.partial(scatter.settle, p) for p in range(THREE)} | {turn: functools.partial(scatter.absorb, turn) for turn in range(SIDE)}
    if parity == TWO:
        for name in plan.get(position, ()):
            steps[name]()
        return
    if parity == THREE:
        @pl.when(position == 5)
        def _():
            for name in plan['late']:
                steps[name]()
        return
    if parity == ZERO:
        @pl.when(position == ZERO)
        def _():
            meet_neighbours(scatter.place)
            scatter.begin()
    for where, names in plan.items():
        if where != 'late' and where < 12:
            @pl.when(position == where)
            def _():
                for name in names:
                    steps[name]()


def no_guest(parity, position):
    pass


def attn_backward(dres, q, k, v, lse, lens, attn_full, bias_rows, mats, causal, lhs_list, g_rows=None, scale=None, gain_row=ZERO, normed=None, inv_std=None, grads=None):
    d_model = q.shape[-ONE]
    n_batch = lens.shape[ZERO]
    n_q, n_k = q.shape[ZERO] // n_batch, k.shape[ZERO] // n_batch
    n_groups = d_model // GROUP
    row = lambda mat: pl.BlockSpec((GROUP, d_model), lambda b, g: (mat * n_groups + g, ZERO))
    q_blk = pl.BlockSpec((n_q, GROUP), lambda b, g: (b, g))
    k_blk = pl.BlockSpec((n_k, GROUP), lambda b, g: (b, g))
    tok = lambda n: pl.BlockSpec((n, d_model), lambda b, g: (b, ZERO))
    n_heads_g = GROUP // HEAD_DIM
    anywhere = pl.BlockSpec(memory_space=pl.ANY)
    in_specs = [pl.BlockSpec(memory_space=pltpu.SMEM), tok(n_q), row(mats[THREE]), anywhere, q_blk, k_blk, k_blk,
                pl.BlockSpec((ONE, ONE, n_heads_g // TWO, TWO, n_q), lambda b, g: (b, g, ZERO, ZERO, ZERO)), pl.BlockSpec(bias_rows.shape, lambda b, g: (ZERO, ZERO))]
    args = [lens, dres, attn_full, attn_full, q, k, v, lse, bias_rows]
    tail_shape = jax.ShapeDtypeStruct((n_batch, 8, d_model), F32)
    out_shape = [jax.ShapeDtypeStruct(q.shape, BF16 if causal else F32)]
    out_specs = [tok(n_q)]
    if not causal:
        late = dict(pipeline_mode=pl.Buffered(ONE))
        in_specs += [pl.BlockSpec((n_q, d_model), lambda b, g: (b, ZERO), **late), pl.BlockSpec((n_q, ONE), lambda b, g: (b, ZERO), **late)]
        args += [normed, inv_std]
        out_shape.append(jax.ShapeDtypeStruct(k.shape, BF16))
        out_specs.append(tok(n_k))
    n_lhs_at = len(args)
    args += list(lhs_list)
    in_specs += [anywhere] * len(lhs_list)
    out_shape += [tail_shape, tail_shape, jax.ShapeDtypeStruct(attn_full.shape, F32)]
    out_specs += [pl.BlockSpec((ONE, 8, GROUP), lambda b, g: (b, ZERO, g)), pl.BlockSpec((ONE, 8, d_model), lambda b, g: (b, ZERO, ZERO)), anywhere]
    held = lambda count, n: pltpu.VMEM((count, n_batch * n, d_model), BF16)
    own = [held(4, n_q), held(TWO, n_q)] if causal else [held(TWO, n_q), held(TWO, n_k), held(ONE, n_q), pltpu.VMEM((n_batch * n_k, d_model), BF16)]
    own += [] if causal else [pltpu.VMEM((n_q, GROUP), BF16)]
    own += [pltpu.VMEM((THREE, d_model, d_model), BF16), pltpu.VMEM((TWO, d_model, d_model), F32), pltpu.SemaphoreType.DMA((6,)), pltpu.SemaphoreType.DMA((TWO,))]
    kernel = functools.partial(attn_bwd_kernel, causal, gain_row, mats)
    params = dict(vmem_limit_bytes=VMEM_BYTES, dimension_semantics=('arbitrary', 'arbitrary'))
    aliases = {}
    if causal:
        args.append(grads)
        in_specs.append(anywhere)
        aliases = {len(args) - ONE: len(out_shape) - ONE}
    else:
        args.append(as_torus(g_rows))
        in_specs.append(anywhere)
        n_rows = args[-ONE].shape[THREE]
        out_shape.append(jax.ShapeDtypeStruct((n_rows, d_model), F32))
        out_specs.append(anywhere)
        params |= dict(collective_id=THREE, has_side_effects=True, vmem_limit_bytes=67043328)
    scratch = own + ([] if causal else Scatter.scratch_shapes([n_rows]))
    n_in, n_out, n_own = len(args), len(out_shape), len(own)

    def body(*refs):
        ins, outs, rest = refs[:n_in], refs[n_in:n_in + n_out], refs[n_in + n_out:]
        lhs_refs, mine = ins[n_lhs_at:-ONE], rest[:n_own]
        if causal:
            dx, sums, tail, grads_ref = outs
            kernel(no_guest, *ins[:n_lhs_at], None, None, lhs_refs, dx, None, sums, tail, grads_ref, mine[ZERO], None, mine[ONE], None, None, *mine[TWO:])
        else:
            dx, dkv, sums, tail, grads_ref, total = outs
            scatter = Scatter(scale, [(ins[-ONE], ZERO, n_rows)], [total], rest[n_own:])
            kernel(functools.partial(scatter_guest, scatter, CROSS_PLAN), *ins[:n_lhs_at], lhs_refs, dx, dkv, sums, tail, grads_ref, *mine)

    return pl.pallas_call(
        body, grid=(n_batch, n_groups), in_specs=in_specs, out_specs=out_specs, out_shape=out_shape, scratch_shapes=scratch, input_output_aliases=aliases,
        compiler_params=pltpu.CompilerParams(**params),
        cost_estimate=pl.CostEstimate(flops=TWO * d_model * d_model * (TWO * q.shape[ZERO] + TWO * k.shape[ZERO]) + 40 * q.shape[ZERO] * n_k * d_model, bytes_accessed=20 * q.shape[ZERO] * d_model, transcendentals=ZERO),
        name='attn_bwd',
    )(*args)


def ffn_kernel(n_blocks, h_ref, dy_ref, up_ref, down_ref, rows_ref, bias_ref, normed_ref, inv_ref,
               y_ref, grad_ref, dres2_ref, tail_ref, upsum_ref, left_all, right_all):
    step = pl.program_id(ZERO)
    block, d_model = h_ref.shape
    n_square = left_all.shape[TWO] // d_model

    @pl.when(step < n_blocks)
    def _():
        rows = pl.ds(pl.multiple_of(step * block, block), block)
        h_b = h_ref[ALL]
        right_all[ZERO, rows, :] = h_b
        up = dot_nt(h_b, up_ref[ALL]) + bias_ref[ALL]
        cdf = 0.5 * (1.0 + lax.erf(up * 0.7071067811865476))
        gelu = (up * cdf).astype(BF16)
        slope = cdf + up * (0.3989422804014327 * jnp.exp(-0.5 * up * up))
        left_all[ONE, rows, :] = gelu
        resid = h_b.astype(F32) + dot(gelu, down_ref[ALL]) + rows_ref[8:9, :]
        y_b, normed3, inv3 = norm_rows(resid, rows_ref[13:14, :], rows_ref[14:15, :])
        y_ref[ALL] = y_b
        dy = dy_ref[ALL].astype(F32)
        d_res3 = norm_rows_bwd(dy, normed3, inv3, rows_ref[13:14, :])
        d_res3_b = d_res3.astype(BF16)
        right_all[ONE, rows, :] = d_res3_b
        d_up = dot_nt(d_res3_b, down_ref[ALL]) * slope
        d_up_b = d_up.astype(BF16)
        left_all[ZERO, rows, :] = d_up_b
        d_h2 = d_res3 + dot(d_up_b, up_ref[ALL])
        normed2 = normed_ref[ALL]
        d_res2 = norm_rows_bwd(d_h2, normed2, inv_ref[ALL], rows_ref[11:12, :])
        dres2_ref[ALL] = d_res2
        tail = jnp.concatenate([col_sum(d_res2), col_sum(d_res3), col_sum(d_h2 * normed2), col_sum(d_h2), col_sum(dy * normed3), col_sum(dy),
                                jnp.zeros((TWO, dy.shape[ONE]), F32)], axis=ZERO)
        up_sum = col_sum(d_up)

        @pl.when(step == ZERO)
        def _():
            tail_ref[ALL] = tail
            upsum_ref[ALL] = up_sum

        @pl.when(step > ZERO)
        def _():
            tail_ref[ALL] += tail
            upsum_ref[ALL] += up_sum

    square = step - n_blocks
    cols = pl.ds(pl.multiple_of(lax.rem(square + TWO * n_square, n_square) * d_model, d_model), d_model)

    @pl.when(square >= ZERO)
    def _():
        which = square // n_square
        grad_ref[ALL] = dot_tn(left_all[which, :, cols], right_all[which])


def ffn_both(h2, dy, ffn_full, bias_rows, up_bias, normed2, inv2, block=256):
    n_tok, d_model = h2.shape
    ffn_dim = ffn_full.shape[ZERO] // TWO
    n_blocks = n_tok // block
    n_steps = n_blocks + ffn_full.shape[ZERO] // d_model
    at = lambda i: jnp.minimum(i, n_blocks - ONE)
    tok = pl.BlockSpec((block, d_model), lambda i: (at(i), ZERO))
    once = lambda shape, idx: pl.BlockSpec(shape, lambda i: idx, pipeline_mode=pl.Buffered(ONE))
    return pl.pallas_call(
        functools.partial(ffn_kernel, n_blocks), grid=(n_steps,),
        in_specs=[tok, tok, once((ffn_dim, d_model), (ZERO, ZERO)), once((ffn_dim, d_model), (ONE, ZERO)), once(bias_rows.shape, (ZERO, ZERO)), once((ONE, ffn_dim), (ZERO, ZERO)),
                  tok, pl.BlockSpec((block, ONE), lambda i: (at(i), ZERO))],
        out_specs=[tok, pl.BlockSpec((d_model, d_model), lambda i: (jnp.maximum(i - n_blocks, ZERO), ZERO)), tok, pl.BlockSpec((8, d_model), lambda i: (ZERO, ZERO)), pl.BlockSpec((ONE, ffn_dim), lambda i: (ZERO, ZERO))],
        out_shape=[jax.ShapeDtypeStruct(h2.shape, BF16), jax.ShapeDtypeStruct(ffn_full.shape, F32), jax.ShapeDtypeStruct(h2.shape, F32),
                   jax.ShapeDtypeStruct((8, d_model), F32), jax.ShapeDtypeStruct((ONE, ffn_dim), F32)],
        scratch_shapes=[pltpu.VMEM((TWO, n_tok, ffn_dim), BF16), pltpu.VMEM((TWO, n_tok, d_model), BF16)],
        compiler_params=pltpu.CompilerParams(vmem_limit_bytes=VMEM_BYTES, dimension_semantics=('arbitrary',)),
        cost_estimate=pl.CostEstimate(flops=12 * n_tok * d_model * ffn_dim, bytes_accessed=30 * n_tok * d_model, transcendentals=ZERO),
        name='ffn_both',
    )(h2, dy, ffn_full, ffn_full, bias_rows, up_bias, normed2, inv2)


CROSS_PLAN = {ONE: (ZERO,), TWO: (ONE,), THREE: (TWO,), 4: (THREE,), 5: (('relay', ZERO),), 9: (('settle', ZERO),), 10: (('relay', ONE),), 'late': (('settle', ONE),), 12: (('relay', TWO),), 13: (('settle', TWO),), 14: ('end',)}


def solution(mesh):
    n_fsdp = mesh.shape['fsdp']
    n_dp = mesh.shape['dp']
    batch_axes = ('dp', 'fsdp')
    act_spec = P(batch_axes, None, None)
    len_spec = P(batch_axes)
    row_spec = P('fsdp', None)
    vec_spec = P('fsdp')

    def device_step(dec_in, enc_out, src_lens, tgt_lens, y_cot, attn_w, ffn_w, vec_params):
        d_model, n_vec = dec_in.shape[TWO], vec_params.shape[ZERO]
        scale = 1.0 / (dec_in.shape[ZERO] * dec_in.shape[ONE] * n_fsdp * n_dp)
        x, enc, dy = (a.reshape(-ONE, d_model) for a in (dec_in, enc_out, y_cot))
        vec_rows = jnp.pad(vec_params.astype(F32), (ZERO, 16 * LANES - n_vec)).reshape(16, LANES)
        attn_tiles, planes, vec_tiles = gather_params(attn_w, ffn_w, vec_rows)
        attn_full = attn_tiles.reshape(-ONE, d_model)
        vec_f = vec_tiles.reshape(n_fsdp, 16, LANES)[:, :TWO].reshape(n_fsdp, TWO * LANES)[:, :n_vec].reshape(-ONE)
        bias_rows = jnp.pad(vec_f[:15 * d_model].reshape(15, d_model), ((ZERO, ONE), (ZERO, ZERO)))
        up_bias = vec_f[15 * d_model:].reshape(ONE, -ONE)
        q1, k1, v1, o1, lse1, h1, normed1, inv1 = attn_forward(x, x, tgt_lens, attn_full, bias_rows, (ZERO, ONE, TWO, THREE), (ZERO, ONE, TWO, THREE, 9), True)
        q2, k2, v2, o2, lse2, h2, normed2, inv2, ffn_tiles = attn_forward(h1, enc, src_lens, attn_full, bias_rows, (4, 5, 6, 7), (4, 5, 6, 7, 11), False, planes, ffn_w.shape[ZERO] * n_fsdp)
        ffn_full = ffn_tiles.reshape(-ONE, d_model)
        y, g_ffn, d_res2, ffn_tail, up_sum = ffn_both(h2, dy, ffn_full, bias_rows, up_bias, normed2, inv2)
        d_res1, d_enc, sums2, tail2, grads, ffn_out = attn_backward(d_res2, q2, k2, v2, lse2, src_lens, attn_full, bias_rows, (4, 5, 6, 7), False, (h1, enc, o2), g_ffn, scale, 9, normed1, inv1)
        d_x, sums1, _, grads = attn_backward(d_res1, q1, k1, v1, lse1, tgt_lens, attn_full, bias_rows, (ZERO, ONE, TWO, THREE), True, (x, o1), grads=grads)
        s1, s2, t2 = jnp.sum(sums1, axis=ZERO), jnp.sum(sums2, axis=ZERO), jnp.sum(tail2, axis=ZERO)
        g_vec = jnp.concatenate([s1[ZERO:THREE].reshape(-ONE), t2[ZERO], s2[ZERO:THREE].reshape(-ONE), ffn_tail[ZERO], ffn_tail[ONE], t2[ONE], t2[TWO], ffn_tail[TWO], ffn_tail[THREE], ffn_tail[4], ffn_tail[5], up_sum[ZERO]])
        g_rows = jnp.pad(g_vec.reshape(n_fsdp, ONE, n_vec), ((ZERO, ZERO), (ZERO, 7), (ZERO, d_model - n_vec))).reshape(n_fsdp * 8, -ONE)
        attn_out, vec_out = scatter_grads(grads, g_rows, scale)
        return y.reshape(dec_in.shape), d_x.reshape(dec_in.shape), d_enc.reshape(enc_out.shape), attn_out, ffn_out, vec_out[ZERO, :n_vec]

    return jax.shard_map(device_step, mesh=mesh, in_specs=(act_spec, act_spec, len_spec, len_spec, act_spec, row_spec, row_spec, vec_spec), out_specs=(act_spec, act_spec, act_spec, row_spec, row_spec, vec_spec), check_vma=False)
```

profile of v0, /device:TPU:1, one launch (start us, length us, event | category | flops | bytes accessed | tf_op | source)
XLA Modules:
  0.0 307.4 jit_solution(9661906664888317950)
XLA Ops:
  0.6 0.0 copy-start.7
  0.6 1.3 bitcast_convert_fusion.vec_ref
  1.9 44.5 %gather_params.1 = (bf16[4,4,4,96,768]{4,3,2,1,0:T(8,128)(2,1)}, bf16[3,4,4,16,768]{4,3,2,1,0:T(8,128)(2,1)}, f32[4,4,4,16,128]{4,3,2,1,0:T(8,128)}) custom-call(bf16[96,768]{1,0:T(8,128)(2,1)} %attn_ref.1, bf16[96,768]{1,0:T(8,128)(2,1)} %ffn_ref.1, f32[16,128]{1,0:T(8,128)} %bitcast_convert_fusion.vec_ref), custom_call_target="tpu_custom_call" | custom-call | flops 1000000000 | bytes 18874368 | tf_op jit(solution)/shard_map/gather_params/pallas_call | solution.py:418
  46.5 1.0 slice.69
  47.4 0.1 slice.54
  47.6 0.0 copy-done.7
  47.6 0.7 slice_select_fusion.bias_ref.rows_ref.refs_7_.refs_8_
  48.3 20.6 %attn_fwd.2 = (bf16[1024,768]{1,0:T(8,128)(2,1)}, bf16[1024,768]{1,0:T(8,128)(2,1)}, bf16[1024,768]{1,0:T(8,128)(2,1)}, bf16[1024,768]{1,0:T(8,128)(2,1)}, f32[2...) custom-call(s32[2]{0:T(128)} %refs_0_.5, ...), custom_call_target="tpu_custom_call" | custom-call | flops 11274289152 | bytes 15728640 | tf_op jit(solution)/shard_map/attn_fwd/pallas_call | solution.py:768
  68.9 29.6 %attn_fwd.3 = (bf16[1024,768]{1,0:T(8,128)(2,1)}, bf16[1536,768]{1,0:T(8,128)(2,1)}, bf16[1536,768]{1,0:T(8,128)(2,1)}, bf16[1024,768]{1,0:T(8,128)(2,1)}, f32[2...) custom-call(s32[2]{0:T(128)} %refs_0_.4, ...), custom_call_target="tpu_custom_call" | custom-call | flops 15703474176 | bytes 15728640 | tf_op jit(solution)/shard_map/attn_fwd/pallas_call | solution.py:768
  98.5 0.1 reshape.80
  98.6 0.6 slice.72
  99.2 44.6 %ffn_both.1 = (bf16[1024,768]{1,0:T(8,128)(2,1)}, f32[6144,768]{1,0:T(8,128)}, f32[1024,768]{1,0:T(8,128)}, f32[8,768]{1,0:T(8,128)}, f32[1,3072]{1,0:T(1,128)}) custom-call(bf16[1024,768]{1,0:T(8,128)(2,1)} %get-tuple-element.46.h_ref, bf16[1024,768]{1,0:T(8,128)(2,1)} %bitcast.35, bf16[6144,768]{1,0:T(8,128)(2,1)} %bitcast.52, bf16[6144,768]{1,0:T(8,128)(2,1)} %bitcast.53, ...), custom_call_target="tpu_custom_call" | custom-call | flops 28991029248 | bytes 23592960 | tf_op jit(solution)/shard_map/ffn_both/pallas_call | solution.py:1050
  143.8 68.6 %attn_bwd.2 = (f32[1024,768]{1,0:T(8,128)}, bf16[1536,768]{1,0:T(8,128)(2,1)}, f32[2,8,768]{2,1,0:T(8,128)}, f32[2,8,768]{2,1,0:T(8,128)}, f32[6144,768]{1,0:T(8,128)}, /*index=5*/f32[96,768]{1,0:T(8,128)}) custom-call(s32[2]{0:T(128)} %refs_0_.4, f32[1024,768]{1,0:T(8,128)} %get-tuple-element.51.refs_1_, bf16[6144,768]{1,0:T(8,128)(2,1)} %bitcast.48, ...), custom_call_target="tpu_custom_call" | custom-call | flops 30198988800 | bytes 15728640 | tf_op jit(solution)/shard_map/attn_bwd/pallas_call | solution.py:981
  212.4 0.0 copy-start.4
  212.4 0.0 copy-start.3
  212.4 0.0 copy-start.5
  212.4 0.0 copy-start.6
  212.4 32.6 %attn_bwd.3 = (bf16[1024,768]{1,0:T(8,128)(2,1)}, f32[2,8,768]{2,1,0:T(8,128)}, f32[2,8,768]{2,1,0:T(8,128)}, f32[6144,768]{1,0:T(8,128)}) custom-call(s32[2]{0:T(128)} %refs_0_.5, f32[1024,768]{1,0:T(8,128)} %get-tuple-element.60.refs_1_, bf16[6144,768]{1,0:T(8,128)(2,1)} %bitcast.50, bf16[6144,768]{1,0:T(8,128)(2,1)} %bitcast.51, ...), custom_call_target="tpu_custom_call", output_to_operand_aliasing={{3}: (11, {})} | custom-call | flops 20937965568 | bytes 15728640 | tf_op jit(solution)/shard_map/attn_bwd/pallas_call | solution.py:981
  245.1 0.8 reduce_sum.27
  245.9 0.0 copy-done.4
  246.0 0.0 copy-done.3
  246.1 0.0 copy-done.5
  246.1 0.1 slice_reduce_fusion.3
  246.3 0.2 reshape.89
  246.5 1.2 pad.15
  247.7 55.6 %scatter_grads.1 = (f32[96,768]{1,0:T(8,128)}, f32[8,768]{1,0:T(8,128)}) custom-call(f32[4,4,4,96,768]{4,3,2,1,0:T(8,128)} %bitcast.23, f32[4,4,4,8,768]{4,3,2,1,0:T(8,128)} %bitcast.24), custom_call_target="tpu_custom_call" | custom-call | flops 1000000000 | bytes 37748736 | tf_op jit(solution)/shard_map/scatter_grads/pallas_call | solution.py:261
  303.3 1.3 slice.68
  304.5 1.4 copy.34
  306.0 0.0 copy-done.2
  306.0 0.7 copy.35
  306.7 0.0 copy-done.1
  306.7 0.7 copy.36
  (26 shorter events, 0.2 us)
Async XLA Ops:
  0.6 47.0 %copy-start.7 = (pred[16]{0:T(512)(128)(4,1)S(1)}, pred[16]{0:T(512)(128)(4,1)}, u32[]{:S(2)}) copy-start(pred[16]{0:T(512)(128)(4,1)} %constant.6.clone.1) | copy-start | bytes 52
  212.4 33.5 %copy-start.4 = (f32[2,8,768]{2,1,0:T(8,128)S(1)}, f32[2,8,768]{2,1,0:T(8,128)}, u32[]{:S(2)}) copy-start(f32[2,8,768]{2,1,0:T(8,128)} %get-tuple-element.71) | copy-start | bytes 147460
  212.4 33.6 %copy-start.3 = (f32[2,8,768]{2,1,0:T(8,128)S(1)}, f32[2,8,768]{2,1,0:T(8,128)}, u32[]{:S(2)}) copy-start(f32[2,8,768]{2,1,0:T(8,128)} %get-tuple-element.72) | copy-start | bytes 147460
  212.4 33.6 %copy-start.5 = (f32[8,768]{1,0:T(8,128)S(1)}, f32[8,768]{1,0:T(8,128)}, u32[]{:S(2)}) copy-start(f32[8,768]{1,0:T(8,128)} %get-tuple-element.73) | copy-start | bytes 73732
  212.4 33.8 %copy-start.6 = (f32[1,3072]{1,0:T(1,128)S(1)}, f32[1,3072]{1,0:T(1,128)}, u32[]{:S(2)}) copy-start(f32[1,3072]{1,0:T(1,128)} %get-tuple-element.74) | copy-start | bytes 36868
  247.7 56.8 %copy-start = (bf16[1536,768]{1,0:T(8,128)(2,1)S(1)}, bf16[1536,768]{1,0:T(8,128)(2,1)}, u32[]{:S(2)}) copy-start(bf16[1536,768]{1,0:T(8,128)(2,1)} %get-tuple-element.68) | copy-start | bytes 7077892
  304.5 1.4 copy-start.2
  304.5 2.1 copy-start.1
where the time goes:
time: 308 us; the launch traced here: 307 us
  Pallas kernels  296 us (96%)
  local copies, waits for them, and re-layouts  7.58 us (2%)
    pallas_call x2, Pallas kernels, attn_backward(): pl.pallas_call(body, grid=(n_batch, n_groups), in_specs=in_specs, out_spe...  101 us
    pallas_call x1, Pallas kernels, scatter_grads(): pl.pallas_call(functools.partial(rs_kernel, scale), in_specs=[anywhere] *...  55.6 us
    pallas_call x2, Pallas kernels, attn_forward(): pl.pallas_call(body, grid=(n_batch, n_groups), in_specs=in_specs, out_spe...  50.2 us
    pallas_call x1, Pallas kernels, ffn_both(): pl.pallas_call(functools.partial(ffn_kernel, n_blocks), grid=(n_steps,),...  44.6 us
    pallas_call x1, Pallas kernels, gather_params(): pl.pallas_call(ag_kernel, in_specs=[vmem] * THREE, out_specs=[pl.BlockSpe...  44.5 us

commit v1 on v0

--- a/solution.py
+++ b/solution.py
@@ -47,38 +47,42 @@
 
 
 class Scatter:
-    def __init__(self, scale, sources, outs, scratch, resident=False):
-        self.scale, self.outs, self.resident = scale, outs, resident
+    def __init__(self, scale, sources, outs, scratch):
+        self.scale, self.outs = scale, outs
         self.sources = [(ref, pl.ds(first, n)) for ref, first, n in sources]
-        (self.acc, g1, d1, g2, d2, g3, d3, self.send_sem, self.recv_sem, self.load_sem, *stage) = scratch
-        self.stage = None if resident else stage[ZERO]
+        (self.acc, g1, d1, g2, d2, g3, d3, self.send_sem, self.recv_sem, self.load_sem, self.stage) = scratch
         self.got, self.far = (g1, g2, g3), (d1, d2, d3)
         self.heights = [n for _, _, n in sources]
         self.offsets = [sum(self.heights[:i]) for i in range(len(sources))]
-        self.height = sum(self.heights)
         self.n_low = self.heights[ZERO] // TWO
         self.core, self.chip, self.place = lax.axis_index('dp'), lax.axis_index('fsdp'), torus_place()
         self.pieces = [(d, colour) for d in (TWO, ONE, THREE, ZERO) for colour in range(COLOURS)]
 
     @staticmethod
-    def scratch_shapes(heights, resident=False):
+    def scratch_shapes(heights):
         h = sum(heights)
         n_low = heights[ZERO] // TWO
         buf = lambda *shape: pltpu.VMEM((COLOURS,) + shape + (LANES,), F32)
         n = Scatter.n_copies(len(heights))
         return [buf(SIDE, SIDE, SIDE, h), buf(TWO, SIDE, SIDE, h), buf(TWO, TWO, SIDE, h), buf(TWO, SIDE, h), buf(TWO, TWO, h), buf(TWO, h), buf(TWO, max(n_low, h - n_low)),
-                pltpu.SemaphoreType.DMA((n,)), pltpu.SemaphoreType.DMA((n,)), pltpu.SemaphoreType.DMA((THREE + COLOURS, len(heights)))] + (
-                    [] if resident else [pltpu.VMEM((STAGES, SIDE, SIDE, h, LANES), F32)])
+                pltpu.SemaphoreType.DMA((n,)), pltpu.SemaphoreType.DMA((n,)), pltpu.SemaphoreType.DMA((THREE + COLOURS, len(heights))),
+                pltpu.VMEM((STAGES, SIDE, SIDE, h, LANES), F32)]
 
     @staticmethod
     def n_copies(n_parts):
         return 12 * n_parts + COLOURS * 18 + COLOURS * n_parts
 
+    def parts(self, colour):
+        return range(len(self.sources) if colour == ZERO else ONE)
+
+    def height(self, colour):
+        return sum(self.heights[i] for i in self.parts(colour))
+
     def remote(self, i, src, dst, device):
         return pltpu.make_async_remote_copy(src_ref=src, dst_ref=dst, send_sem=self.send_sem.at[i], recv_sem=self.recv_sem.at[i], device_id=device, device_id_type=MESH_ID)
 
-    def columns(self, of_core, colour):
-        return pl.ds(pl.multiple_of((of_core * COLOURS + colour) * LANES, LANES), LANES)
+    def columns(self, of_core, colour, part=ZERO):
+        return pl.ds(pl.multiple_of((of_core * COLOURS + colour if part == ZERO else of_core) * LANES, LANES), LANES)
 
     def slot(self, d, colour):
         dim = DIM_ORDER[colour][ZERO]
@@ -91,21 +95,19 @@
 
     def swaps(self, piece):
         d, colour = self.pieces[piece]
-        where, cols = self.slot(d, colour), self.columns(ONE - self.core, colour)
+        where = self.slot(d, colour)
         n = len(self.sources)
-        return [self.remote(piece * n + i, src.at[where + (rows, cols)], self.acc.at[(colour,) + where + (self.rows_of(i), slice(None))], (ONE - self.core, self.chip))
-                for i, (src, rows) in enumerate(self.sources)]
+        return [self.remote(piece * n + i, self.sources[i][ZERO].at[where + (self.sources[i][ONE], self.columns(ONE - self.core, colour, i))],
+                            self.acc.at[(colour,) + where + (self.rows_of(i), slice(None))], (ONE - self.core, self.chip)) for i in self.parts(colour)]
 
     def loads(self, piece):
         d, colour = self.pieces[piece]
-        where, cols = self.slot(d, colour), self.columns(self.core, colour)
-        if self.resident:
-            return []
-        return [pltpu.make_async_copy(src.at[where + (rows, cols)], self.stage.at[piece % STAGES, :, :, self.rows_of(i), :], self.load_sem.at[piece % STAGES, i])
-                for i, (src, rows) in enumerate(self.sources)]
-
-    def split_rows(self, half):
-        return pl.ds(ZERO, self.n_low) if half == ZERO else pl.ds(self.n_low, self.height - self.n_low)
+        where, buf = self.slot(d, colour), piece % STAGES
+        return [pltpu.make_async_copy(self.sources[i][ZERO].at[where + (self.sources[i][ONE], self.columns(self.core, colour, i))],
+                                      self.stage.at[buf, :, :, self.rows_of(i), :], self.load_sem.at[buf, i]) for i in self.parts(colour)]
+
+    def split_rows(self, colour, half):
+        return pl.ds(ZERO, self.n_low) if half == ZERO else pl.ds(self.n_low, self.height(colour) - self.n_low)
 
     def block(self, colour, phase, d, half=None):
         order = DIM_ORDER[colour]
@@ -115,17 +117,23 @@
         where[order[phase]] = lax.rem(self.place[order[phase]] + d, SIDE)
         for i, rest in enumerate(sorted(order[phase + ONE:])):
             where[rest] = slice(None) if half is None or i > ZERO else pl.ds(TWO * half, TWO)
-        rows = self.split_rows(half) if phase == TWO and half is not None else slice(None)
+        rows = self.split_rows(colour, half) if phase == TWO and half is not None else pl.ds(ZERO, self.height(colour))
         return self.acc.at[(colour,) + tuple(where) + (rows, slice(None))]
 
     def got_half(self, colour, phase, direction, half):
-        where = self.split_rows(half) if phase == TWO else pl.ds(TWO * half, TWO)
-        return self.got[phase].at[colour, direction, where]
+        if phase == TWO:
+            return self.got[phase].at[colour, direction, self.split_rows(colour, half), :]
+        return self.got_all(colour, phase, direction, pl.ds(TWO * half, TWO))
+
+    def got_all(self, colour, phase, direction, which=slice(None)):
+        rows = (pl.ds(ZERO, self.height(colour)), slice(None))
+        blocks = ((which, slice(None)), (which,), ())[phase]
+        return self.got[phase].at[(colour, direction) + blocks + rows]
 
     def far_part(self, colour, phase, direction):
         if phase == TWO:
-            return self.far[phase].at[colour, direction, pl.ds(ZERO, self.n_low if direction == ZERO else self.height - self.n_low), :]
-        return self.far[phase].at[colour, direction]
+            return self.far[phase].at[colour, direction, pl.ds(ZERO, self.n_low if direction == ZERO else self.height(colour) - self.n_low), :]
+        return self.far[phase].at[(colour, direction) + (slice(None),) * (TWO - phase) + (pl.ds(ZERO, self.height(colour)), slice(None))]
 
     def ring(self, colour, phase, direction):
         shift = ONE - TWO * direction
@@ -140,8 +148,7 @@
         n = len(self.sources)
         base = 12 * n + COLOURS * 18 + colour * n
         done = self.acc.at[colour, self.place[ZERO], self.place[ONE], self.place[TWO]]
-        cols = self.columns(self.core, colour)
-        pairs = [(done.at[self.rows_of(i), :], out.at[:, cols]) for i, out in enumerate(self.outs)]
+        pairs = [(done.at[self.rows_of(i), :], self.outs[i].at[:, self.columns(self.core, colour, i)]) for i in self.parts(colour)]
         return [(self.remote(base + i, src, dst, (ONE - self.core, self.chip)), pltpu.make_async_copy(src, dst, self.load_sem.at[THREE + colour, i])) for i, (src, dst) in enumerate(pairs)]
 
     def add_into(self, dst, sources, n_lead):
@@ -176,12 +183,8 @@
                 copy.wait()
             for copy in self.swaps(piece):
                 copy.wait_recv()
-            where = self.slot(d, colour)
-            if self.resident:
-                for i, (src, rows) in enumerate(self.sources):
-                    self.add_into(self.acc.at[(colour,) + where + (self.rows_of(i), slice(None))], [src.at[where + (rows, self.columns(self.core, colour))]], TWO)
-            else:
-                self.add_into(self.acc.at[(colour,) + where], [self.stage.at[piece % STAGES]], TWO)
+            rows = (pl.ds(ZERO, self.height(colour)), slice(None))
+            self.add_into(self.acc.at[(colour,) + self.slot(d, colour) + rows], [self.stage.at[(piece % STAGES, slice(None), slice(None)) + rows]], TWO)
             if piece + STAGES < len(self.pieces):
                 for copy in self.loads(piece + STAGES):
                     copy.start()
@@ -206,13 +209,13 @@
                 _, own, fed = self.ring(colour, phase, direction)
                 own.wait_recv()
                 fed.wait_recv()
-            self.add_into(self.block(colour, phase, ZERO), [self.got[phase].at[colour, direction] for direction in range(TWO)], TWO - phase)
+            self.add_into(self.block(colour, phase, ZERO), [self.got_all(colour, phase, direction) for direction in range(TWO)], TWO - phase)
             if phase < TWO:
                 for kind in range(TWO):
                     for direction in range(TWO):
                         self.ring(colour, phase + ONE, direction)[kind].start()
             else:
-                done = self.acc.at[colour, self.place[ZERO], self.place[ONE], self.place[TWO]]
+                done = self.block(colour, TWO, ZERO)
                 done[ALL] = done[ALL] * self.scale
                 for give, keep in self.gives(colour):
                     keep.start()
@@ -234,39 +237,75 @@
                         copy.wait_send()
 
 
-def rs_kernel(scale, *refs):
-    scatter = Scatter(scale, [(ref, ZERO, ref.shape[THREE]) for ref in refs[:TWO]], refs[TWO:4], refs[4:])
+def rs_kernel(scale, mats, g_ref, vec_ref, w_all, dres_ref, self_ref, cross_ref, out_ref, vec_out, dx_out, denc_out,
+              w_v, dres_v, self_v, cross_v, dx_v, denc_v, load_sem, *scratch):
+    scatter = Scatter(scale, [(ref, ZERO, ref.shape[THREE]) for ref in (g_ref, vec_ref)], [out_ref, vec_out], scratch)
+    d_model = w_v.shape[ONE]
+    step = 256
+    loads = [pltpu.make_async_copy(w_all.at[pl.ds(mat * d_model, d_model), :], w_v.at[i], load_sem.at[i]) for i, mat in enumerate(mats)]
+    loads += [pltpu.make_async_copy(src, dst, load_sem.at[len(mats) + i]) for i, (src, dst) in enumerate(((dres_ref, dres_v), (self_ref, self_v), (cross_ref, cross_v)))]
+    stores = [pltpu.make_async_copy(src, dst, load_sem.at[len(mats) + THREE + i]) for i, (src, dst) in enumerate(((dx_v, dx_out), (denc_v, denc_out)))]
+
+    def input_grads():
+        for copy in loads:
+            copy.wait()
+
+        def decoder(i, _):
+            rows = pl.ds(pl.multiple_of(i * step, step), step)
+            total = dres_v[rows, :]
+            for n in range(THREE):
+                total = total + dot_nt(self_v[n, rows, :], w_v[n])
+            dx_v[rows, :] = total.astype(BF16)
+            return ZERO
+
+        def encoder(i, _):
+            rows = pl.ds(pl.multiple_of(i * step, step), step)
+            denc_v[rows, :] = (dot_nt(cross_v[ZERO, rows, :], w_v[THREE]) + dot_nt(cross_v[ONE, rows, :], w_v[4])).astype(BF16)
+            return ZERO
+
+        lax.fori_loop(ZERO, dx_v.shape[ZERO] // step, decoder, ZERO)
+        stores[ZERO].start()
+        lax.fori_loop(ZERO, denc_v.shape[ZERO] // step, encoder, ZERO)
+        stores[ONE].start()
+
     meet_neighbours(scatter.place)
     scatter.begin()
+    for copy in loads:
+        copy.start()
     for turn in range(THREE):
         scatter.absorb(turn)
     scatter.relay(ZERO)
     scatter.absorb(THREE)
+    input_grads()
     scatter.settle(ZERO)
     for phase in (ONE, TWO):
         scatter.relay(phase)
         scatter.settle(phase)
     scatter.end()
+    for copy in stores:
+        copy.wait()
 
 
 def as_torus(rows):
     return rows.reshape(SIDE, SIDE, SIDE, rows.shape[ZERO] // SIDE ** THREE, rows.shape[ONE])
 
 
-def scatter_grads(g_attn, g_vec, scale):
+def scatter_grads(g_attn, g_vec, scale, attn_full, mats, d_res, d_self, d_cross):
     sources = [as_torus(g_attn), as_torus(g_vec)]
     heights = [src.shape[THREE] for src in sources]
-    width = g_attn.shape[ONE]
+    d_model = g_attn.shape[ONE]
     anywhere = pl.BlockSpec(memory_space=pl.ANY)
+    dx_shape, denc_shape = d_self.shape[ONE:], d_cross.shape[ONE:]
     return pl.pallas_call(
-        functools.partial(rs_kernel, scale),
-        in_specs=[anywhere] * TWO, out_specs=[anywhere] * TWO,
-        out_shape=[jax.ShapeDtypeStruct((h, width), F32) for h in heights],
-        scratch_shapes=Scatter.scratch_shapes(heights),
+        functools.partial(rs_kernel, scale, mats),
+        in_specs=[anywhere] * 6, out_specs=[anywhere] * 4,
+        out_shape=[jax.ShapeDtypeStruct((h, src.shape[4]), F32) for h, src in zip(heights, sources)] + [jax.ShapeDtypeStruct(dx_shape, BF16), jax.ShapeDtypeStruct(denc_shape, BF16)],
+        scratch_shapes=[pltpu.VMEM((len(mats), d_model, d_model), BF16), pltpu.VMEM(d_res.shape, F32), pltpu.VMEM(d_self.shape, BF16), pltpu.VMEM(d_cross.shape, BF16),
+                        pltpu.VMEM(dx_shape, BF16), pltpu.VMEM(denc_shape, BF16), pltpu.SemaphoreType.DMA((len(mats) + 5,))] + Scatter.scratch_shapes(heights),
         compiler_params=pltpu.CompilerParams(collective_id=ONE, has_side_effects=True, vmem_limit_bytes=VMEM_BYTES),
-        cost_estimate=pl.CostEstimate(flops=10 ** 9, bytes_accessed=8 * width * g_attn.shape[ZERO], transcendentals=ZERO),
+        cost_estimate=pl.CostEstimate(flops=10 ** 9, bytes_accessed=8 * d_model * g_attn.shape[ZERO], transcendentals=ZERO),
         name='scatter_grads',
-    )(*sources)
+    )(*sources, attn_full, d_res, d_self, d_cross)
 
 
 class Gather:
@@ -774,13 +813,14 @@
 
 
 def attn_bwd_kernel(causal, gain_row, mats, guest, lens_ref, dres_ref, wo_ref, w_all, q_ref, k_ref, v_ref, lse_ref,
-                    rows_ref, normed_ref, inv_ref, lhs_refs, dx_ref, dkv_ref, sums_ref, tail_ref, grads_ref,
+                    rows_ref, normed_ref, inv_ref, lhs_refs, rows_out, dres_out, sums_ref, tail_ref, grads_ref,
                     rhs_q, rhs_k, lhs_q, lhs_k, do_v, w_v, grad_v, load_sem, store_sem):
     sample, group = pl.program_id(ZERO), pl.program_id(ONE)
-    d_model = w_v.shape[ONE]
+    d_model = wo_ref.shape[ONE]
     n_q, n_k = q_ref.shape[ZERO], k_ref.shape[ZERO]
     last = pl.num_programs(ONE) - ONE
-    fetches = [pltpu.make_async_copy(w_all.at[pl.ds(mat * d_model, d_model), :], w_v.at[i], load_sem.at[i]) for i, mat in enumerate(mats[:THREE])]
+    fetches = [] if causal else [pltpu.make_async_copy(w_all.at[pl.ds(mats[ZERO] * d_model, d_model), :], w_v, load_sem.at[ZERO])]
+    hand_on = pltpu.make_async_copy(rhs_q.at[pl.ds(ZERO, THREE)] if causal else rhs_k, rows_out, load_sem.at[ONE])
     dk_all, dv_all = (rhs_q.at[ONE], rhs_q.at[TWO]) if causal else (rhs_k.at[ZERO], rhs_k.at[ONE])
     d_all, dres_all = rhs_q.at[ZERO], rhs_q.at[THREE if causal else ONE]
     places = (lhs_q.at[ZERO], lhs_q.at[ONE]) if causal else (lhs_q.at[ZERO], lhs_k, lhs_q.at[ZERO])
@@ -822,31 +862,28 @@
     def _():
         dres_all[q_rows, :] = dres_ref[ALL].astype(BF16)
 
-    @pl.when((sample == ZERO) & (group == last))
-    def _():
-        for fetch in fetches:
-            fetch.wait()
-
     guest(THREE, turn)
-
-    @pl.when(group == last)
-    def _():
-        d_kv = dot_nt(dk_all[k_rows, :], w_v[ONE]) + dot_nt(dv_all[k_rows, :], w_v[TWO])
-        d_h = dres_ref[ALL] + dot_nt(d_all[q_rows, :], w_v[ZERO])
-        if causal:
-            dx_ref[ALL] = (d_h + d_kv).astype(BF16)
-            tail_ref[ALL] = jnp.zeros_like(tail_ref)
-        else:
-            dkv_ref[ALL] = d_kv.astype(BF16)
+    if causal:
+        tail_ref[ALL] = jnp.zeros_like(tail_ref)
+    else:
+        @pl.when((sample == ZERO) & (group == last))
+        def _():
+            for fetch in fetches:
+                fetch.wait()
+
+        @pl.when(group == last)
+        def _():
+            d_h = dres_ref[ALL] + dot_nt(d_all[q_rows, :], w_v[ALL])
             normed = normed_ref[ALL]
             d_resid = norm_rows_bwd(d_h, normed, inv_ref[ALL], rows_ref[gain_row:gain_row + ONE, :])
-            dx_ref[ALL] = d_resid
+            dres_out[ALL] = d_resid
             tail_ref[ZERO, ZERO:ONE, :] = col_sum(d_resid)
             tail_ref[ZERO, ONE:TWO, :] = col_sum(d_h * normed)
             tail_ref[ZERO, TWO:THREE, :] = col_sum(d_h)
 
     @pl.when(turn == pl.num_programs(ZERO) * pl.num_programs(ONE) - ONE)
     def _():
+        hand_on.start()
         guest(TWO, 12)
         lhs_fetch(ZERO).wait()
         if causal:
@@ -886,6 +923,7 @@
             guest(TWO, 14)
         for buf in range(TWO):
             store(buf, mats[ZERO]).wait()
+        hand_on.wait()
 
 
 def scatter_guest(scatter, plan, parity, position):
@@ -933,14 +971,14 @@
                 pl.BlockSpec((ONE, ONE, n_heads_g // TWO, TWO, n_q), lambda b, g: (b, g, ZERO, ZERO, ZERO)), pl.BlockSpec(bias_rows.shape, lambda b, g: (ZERO, ZERO))]
     args = [lens, dres, attn_full, attn_full, q, k, v, lse, bias_rows]
     tail_shape = jax.ShapeDtypeStruct((n_batch, 8, d_model), F32)
-    out_shape = [jax.ShapeDtypeStruct(q.shape, BF16 if causal else F32)]
-    out_specs = [tok(n_q)]
+    out_shape = [jax.ShapeDtypeStruct((THREE,) + q.shape if causal else (TWO,) + k.shape, BF16)]
+    out_specs = [anywhere]
     if not causal:
         late = dict(pipeline_mode=pl.Buffered(ONE))
         in_specs += [pl.BlockSpec((n_q, d_model), lambda b, g: (b, ZERO), **late), pl.BlockSpec((n_q, ONE), lambda b, g: (b, ZERO), **late)]
         args += [normed, inv_std]
-        out_shape.append(jax.ShapeDtypeStruct(k.shape, BF16))
-        out_specs.append(tok(n_k))
+        out_shape.append(jax.ShapeDtypeStruct(q.shape, F32))
+        out_specs.append(tok(n_q))
     n_lhs_at = len(args)
     args += list(lhs_list)
     in_specs += [anywhere] * len(lhs_list)
@@ -949,7 +987,8 @@
     held = lambda count, n: pltpu.VMEM((count, n_batch * n, d_model), BF16)
     own = [held(4, n_q), held(TWO, n_q)] if causal else [held(TWO, n_q), held(TWO, n_k), held(ONE, n_q), pltpu.VMEM((n_batch * n_k, d_model), BF16)]
     own += [] if causal else [pltpu.VMEM((n_q, GROUP), BF16)]
-    own += [pltpu.VMEM((THREE, d_model, d_model), BF16), pltpu.VMEM((TWO, d_model, d_model), F32), pltpu.SemaphoreType.DMA((6,)), pltpu.SemaphoreType.DMA((TWO,))]
+    own += [] if causal else [pltpu.VMEM((d_model, d_model), BF16)]
+    own += [pltpu.VMEM((TWO, d_model, d_model), F32), pltpu.SemaphoreType.DMA((6,)), pltpu.SemaphoreType.DMA((TWO,))]
     kernel = functools.partial(attn_bwd_kernel, causal, gain_row, mats)
     params = dict(vmem_limit_bytes=VMEM_BYTES, dimension_semantics=('arbitrary', 'arbitrary'))
     aliases = {}
@@ -971,12 +1010,12 @@
         ins, outs, rest = refs[:n_in], refs[n_in:n_in + n_out], refs[n_in + n_out:]
         lhs_refs, mine = ins[n_lhs_at:-ONE], rest[:n_own]
         if causal:
-            dx, sums, tail, grads_ref = outs
-            kernel(no_guest, *ins[:n_lhs_at], None, None, lhs_refs, dx, None, sums, tail, grads_ref, mine[ZERO], None, mine[ONE], None, None, *mine[TWO:])
+            rows_out, sums, tail, grads_ref = outs
+            kernel(no_guest, *ins[:n_lhs_at], None, None, lhs_refs, rows_out, None, sums, tail, grads_ref, mine[ZERO], None, mine[ONE], None, None, None, *mine[TWO:])
         else:
-            dx, dkv, sums, tail, grads_ref, total = outs
+            rows_out, dres_out, sums, tail, grads_ref, total = outs
             scatter = Scatter(scale, [(ins[-ONE], ZERO, n_rows)], [total], rest[n_own:])
-            kernel(functools.partial(scatter_guest, scatter, CROSS_PLAN), *ins[:n_lhs_at], lhs_refs, dx, dkv, sums, tail, grads_ref, *mine)
+            kernel(functools.partial(scatter_guest, scatter, CROSS_PLAN), *ins[:n_lhs_at], lhs_refs, rows_out, dres_out, sums, tail, grads_ref, *mine)
 
     return pl.pallas_call(
         body, grid=(n_batch, n_groups), in_specs=in_specs, out_specs=out_specs, out_shape=out_shape, scratch_shapes=scratch, input_output_aliases=aliases,
@@ -1087,12 +1126,12 @@
         q2, k2, v2, o2, lse2, h2, normed2, inv2, ffn_tiles = attn_forward(h1, enc, src_lens, attn_full, bias_rows, (4, 5, 6, 7), (4, 5, 6, 7, 11), False, planes, ffn_w.shape[ZERO] * n_fsdp)
         ffn_full = ffn_tiles.reshape(-ONE, d_model)
         y, g_ffn, d_res2, ffn_tail, up_sum = ffn_both(h2, dy, ffn_full, bias_rows, up_bias, normed2, inv2)
-        d_res1, d_enc, sums2, tail2, grads, ffn_out = attn_backward(d_res2, q2, k2, v2, lse2, src_lens, attn_full, bias_rows, (4, 5, 6, 7), False, (h1, enc, o2), g_ffn, scale, 9, normed1, inv1)
-        d_x, sums1, _, grads = attn_backward(d_res1, q1, k1, v1, lse1, tgt_lens, attn_full, bias_rows, (ZERO, ONE, TWO, THREE), True, (x, o1), grads=grads)
+        d_cross, d_res1, sums2, tail2, grads, ffn_out = attn_backward(d_res2, q2, k2, v2, lse2, src_lens, attn_full, bias_rows, (4, 5, 6, 7), False, (h1, enc, o2), g_ffn, scale, 9, normed1, inv1)
+        d_self, sums1, _, grads = attn_backward(d_res1, q1, k1, v1, lse1, tgt_lens, attn_full, bias_rows, (ZERO, ONE, TWO, THREE), True, (x, o1), grads=grads)
         s1, s2, t2 = jnp.sum(sums1, axis=ZERO), jnp.sum(sums2, axis=ZERO), jnp.sum(tail2, axis=ZERO)
         g_vec = jnp.concatenate([s1[ZERO:THREE].reshape(-ONE), t2[ZERO], s2[ZERO:THREE].reshape(-ONE), ffn_tail[ZERO], ffn_tail[ONE], t2[ONE], t2[TWO], ffn_tail[TWO], ffn_tail[THREE], ffn_tail[4], ffn_tail[5], up_sum[ZERO]])
-        g_rows = jnp.pad(g_vec.reshape(n_fsdp, ONE, n_vec), ((ZERO, ZERO), (ZERO, 7), (ZERO, d_model - n_vec))).reshape(n_fsdp * 8, -ONE)
-        attn_out, vec_out = scatter_grads(grads, g_rows, scale)
+        g_rows = jnp.pad(g_vec.reshape(n_fsdp, ONE, n_vec), ((ZERO, ZERO), (ZERO, 7), (ZERO, TWO * LANES - n_vec))).reshape(n_fsdp * 8, -ONE)
+        attn_out, vec_out, d_x, d_enc = scatter_grads(grads, g_rows, scale, attn_full, (ZERO, ONE, TWO, 5, 6), d_res1, d_self, d_cross)
         return y.reshape(dec_in.shape), d_x.reshape(dec_in.shape), d_enc.reshape(enc_out.shape), attn_out, ffn_out, vec_out[ZERO, :n_vec]
 
     return jax.shard_map(device_step, mesh=mesh, in_specs=(act_spec, act_spec, len_spec, len_spec, act_spec, row_spec, row_spec, vec_spec), out_specs=(act_spec, act_spec, act_spec, row_spec, row_spec, vec_spec), check_vma=False)

time: 308 us -> 302 us (0.981)
  Pallas kernels: 296 us -> 288 us
    pallas_call x2, Pallas kernels: 101 us -> 93.7 us  [attn_backward(): pl.pallas_call(body, grid=(n_batch, n_groups), in_specs=in_specs, out_spe...]
where the time goes in v1:
time: 302 us
  Pallas kernels  288 us (95%)
  local copies, waits for them, and re-layouts  9.97 us (3%)
    pallas_call x2, Pallas kernels, attn_backward(): pl.pallas_call(body, grid=(n_batch, n_groups), in_specs=in_specs, out_spe...  93.7 us
    pallas_call x1, Pallas kernels, scatter_grads(): pl.pallas_call(functools.partial(rs_kernel, scale, mats), in_specs=[anywh...  55 us
    pallas_call x2, Pallas kernels, attn_forward(): pl.pallas_call(body, grid=(n_batch, n_groups), in_specs=in_specs, out_spe...  50.2 us
    pallas_call x1, Pallas kernels, ffn_both(): pl.pallas_call(functools.partial(ffn_kernel, n_blocks), grid=(n_steps,),...  44.5 us
    pallas_call x1, Pallas kernels, gather_params(): pl.pallas_call(ag_kernel, in_specs=[vmem] * THREE, out_specs=[pl.BlockSpe...  44.5 us

profile of v1, /device:TPU:1, one launch (start us, length us, event | category | flops | bytes accessed | tf_op | source)
XLA Modules:
  0.0 301.7 jit_solution(18101227565875470245)
XLA Ops:
  0.6 0.0 copy-start.7
  0.6 1.3 bitcast_convert_fusion.vec_ref
  1.9 44.5 %gather_params.1 = (bf16[4,4,4,96,768]{4,3,2,1,0:T(8,128)(2,1)}, bf16[3,4,4,16,768]{4,3,2,1,0:T(8,128)(2,1)}, f32[4,4,4,16,128]{4,3,2,1,0:T(8,128)}) custom-call(bf16[96,768]{1,0:T(8,128)(2,1)} %attn_ref.1, bf16[96,768]{1,0:T(8,128)(2,1)} %ffn_ref.1, f32[16,128]{1,0:T(8,128)} %bitcast_convert_fusion.vec_ref), custom_call_target="tpu_custom_call" | custom-call | flops 1000000000 | bytes 18874368 | tf_op jit(solution)/shard_map/gather_params/pallas_call | solution.py:457
  46.5 1.0 slice.69
  47.4 0.1 slice.54
  47.6 0.0 copy-done.7
  47.6 0.7 slice_select_fusion.bias_ref.rows_ref.refs_7_.refs_8_
  48.3 20.7 %attn_fwd.2 = (bf16[1024,768]{1,0:T(8,128)(2,1)}, bf16[1024,768]{1,0:T(8,128)(2,1)}, bf16[1024,768]{1,0:T(8,128)(2,1)}, bf16[1024,768]{1,0:T(8,128)(2,1)}, f32[2...) custom-call(s32[2]{0:T(128)} %refs_0_.5, ...), custom_call_target="tpu_custom_call" | custom-call | flops 11274289152 | bytes 15728640 | tf_op jit(solution)/shard_map/attn_fwd/pallas_call | solution.py:807
  69.0 29.5 %attn_fwd.3 = (bf16[1024,768]{1,0:T(8,128)(2,1)}, bf16[1536,768]{1,0:T(8,128)(2,1)}, bf16[1536,768]{1,0:T(8,128)(2,1)}, bf16[1024,768]{1,0:T(8,128)(2,1)}, f32[2...) custom-call(s32[2]{0:T(128)} %refs_0_.4, ...), custom_call_target="tpu_custom_call" | custom-call | flops 15703474176 | bytes 15728640 | tf_op jit(solution)/shard_map/attn_fwd/pallas_call | solution.py:807
  98.5 0.1 reshape.80
  98.6 0.6 slice.72
  99.2 44.5 %ffn_both.1 = (bf16[1024,768]{1,0:T(8,128)(2,1)}, f32[6144,768]{1,0:T(8,128)}, f32[1024,768]{1,0:T(8,128)}, f32[8,768]{1,0:T(8,128)}, f32[1,3072]{1,0:T(1,128)}) custom-call(bf16[1024,768]{1,0:T(8,128)(2,1)} %get-tuple-element.48.h_ref, bf16[1024,768]{1,0:T(8,128)(2,1)} %bitcast.49, bf16[6144,768]{1,0:T(8,128)(2,1)} %bitcast.54, bf16[6144,768]{1,0:T(8,128)(2,1)} %bitcast.55, ...), custom_call_target="tpu_custom_call" | custom-call | flops 28991029248 | bytes 23592960 | tf_op jit(solution)/shard_map/ffn_both/pallas_call | solution.py:1089
  143.8 65.4 %attn_bwd.2 = (bf16[2,1536,768]{2,1,0:T(8,128)(2,1)}, f32[1024,768]{1,0:T(8,128)}, f32[2,8,768]{2,1,0:T(8,128)}, f32[2,8,768]{2,1,0:T(8,128)}, f32[6144,768]{1,0:T(8,128)}, /*index=5*/f32[96,768]{1,0:T(8,128)}) custom-call(s32[2]{0:T(128)} %refs_0_.4, f32[1024,768]{1,0:T(8,128)} %get-tuple-element.53.refs_1_, bf16[6144,768]{1,0:T(8,128)(2,1)} %bitcast.32, ...), custom_call_target="tpu_custom_call" | custom-call | flops 30198988800 | bytes 15728640 | tf_op jit(solution)/shard_map/attn_bwd/pallas_call | solution.py:1020
  209.2 0.0 copy-start.4
  209.2 0.0 copy-start.3
  209.2 0.0 copy-start.5
  209.2 0.0 copy-start.6
  209.2 28.2 %attn_bwd.3 = (bf16[3,1024,768]{2,1,0:T(8,128)(2,1)}, f32[2,8,768]{2,1,0:T(8,128)}, f32[2,8,768]{2,1,0:T(8,128)}, f32[6144,768]{1,0:T(8,128)}) custom-call(s32[2]{0:T(128)} %refs_0_.5, f32[1024,768]{1,0:T(8,128)} %get-tuple-element.62.refs_1_.dres_ref, bf16[6144,768]{1,0:T(8,128)(2,1)} %bitcast.34, ...), custom_call_target="tpu_custom_call", output_to_operand_aliasing={{3}: (11, {})} | custom-call | flops 20937965568 | bytes 15728640 | tf_op jit(solution)/shard_map/attn_bwd/pallas_call | solution.py:1020
  237.5 0.8 reduce_sum.27
  238.3 0.0 copy-done.4
  238.4 0.0 copy-done.3
  238.5 0.0 copy-done.5
  238.5 0.1 slice_reduce_fusion.3
  238.7 0.2 reshape.87
  238.9 0.8 pad.15
  239.7 55.0 %scatter_grads.1 = (f32[96,768]{1,0:T(8,128)}, f32[8,256]{1,0:T(8,128)}, bf16[1024,768]{1,0:T(8,128)(2,1)}, bf16[1536,768]{1,0:T(8,128)(2,1)}) custom-call(f32[4,4,4,96,768]{4,3,2,1,0:T(8,128)} %bitcast.23, f32[4,4,4,8,256]{4,3,2,1,0:T(8,128)} %bitcast.38, bf16[6144,768]{1,0:T(8,128)(2,1)} %bitcast.36, f32[1024,768]{1,0:T(8,128)} %get-tuple-element.62.refs_1_.dres_ref, ...), custom_call_target="tpu_custom_call" | custom-call | flops 1000000000 | bytes 37748736 | tf_op jit(solution)/shard_map/scatter_grads/pallas_call | solution.py:299
  294.8 1.4 slice.68
  296.2 2.7 copy.35
  298.8 1.4 copy.36
  300.2 0.0 copy-done.2
  300.2 0.7 copy.37
  301.0 0.7 copy.38
  (27 shorter events, 0.2 us)
Async XLA Ops:
  0.6 46.9 %copy-start.7 = (pred[16]{0:T(512)(128)(4,1)S(1)}, pred[16]{0:T(512)(128)(4,1)}, u32[]{:S(2)}) copy-start(pred[16]{0:T(512)(128)(4,1)} %constant.6.clone.1) | copy-start | bytes 52
  209.2 29.1 %copy-start.4 = (f32[2,8,768]{2,1,0:T(8,128)S(1)}, f32[2,8,768]{2,1,0:T(8,128)}, u32[]{:S(2)}) copy-start(f32[2,8,768]{2,1,0:T(8,128)} %get-tuple-element.71) | copy-start | bytes 147460
  209.2 29.2 %copy-start.3 = (f32[2,8,768]{2,1,0:T(8,128)S(1)}, f32[2,8,768]{2,1,0:T(8,128)}, u32[]{:S(2)}) copy-start(f32[2,8,768]{2,1,0:T(8,128)} %get-tuple-element.72) | copy-start | bytes 147460
  209.2 29.3 %copy-start.5 = (f32[8,768]{1,0:T(8,128)S(1)}, f32[8,768]{1,0:T(8,128)}, u32[]{:S(2)}) copy-start(f32[8,768]{1,0:T(8,128)} %get-tuple-element.73) | copy-start | bytes 73732
  209.2 29.4 %copy-start.6 = (f32[1,3072]{1,0:T(1,128)S(1)}, f32[1,3072]{1,0:T(1,128)}, u32[]{:S(2)}) copy-start(f32[1,3072]{1,0:T(1,128)} %get-tuple-element.74) | copy-start | bytes 36868
  294.7 4.1 %copy-start = (bf16[1536,768]{1,0:T(8,128)(2,1)S(1)}, bf16[1536,768]{1,0:T(8,128)(2,1)}, u32[]{:S(2)}) copy-start(bf16[1536,768]{1,0:T(8,128)(2,1)} %get-tuple-element.78) | copy-start | bytes 7077892
  298.8 1.4 copy-start.2
  298.8 2.1 copy-start.1

commit v2 on v1

--- a/solution.py
+++ b/solution.py
@@ -237,14 +237,13 @@
                         copy.wait_send()
 
 
-def rs_kernel(scale, mats, g_ref, vec_ref, w_all, dres_ref, self_ref, cross_ref, out_ref, vec_out, dx_out, denc_out,
-              w_v, dres_v, self_v, cross_v, dx_v, denc_v, load_sem, *scratch):
+def rs_kernel(scale, mats, g_ref, vec_ref, w_all, dres_ref, self_ref, cross_ref, out_ref, vec_out, dx_v, denc_v,
+              w_v, dres_v, self_v, cross_v, load_sem, *scratch):
     scatter = Scatter(scale, [(ref, ZERO, ref.shape[THREE]) for ref in (g_ref, vec_ref)], [out_ref, vec_out], scratch)
     d_model = w_v.shape[ONE]
     step = 256
     loads = [pltpu.make_async_copy(w_all.at[pl.ds(mat * d_model, d_model), :], w_v.at[i], load_sem.at[i]) for i, mat in enumerate(mats)]
     loads += [pltpu.make_async_copy(src, dst, load_sem.at[len(mats) + i]) for i, (src, dst) in enumerate(((dres_ref, dres_v), (self_ref, self_v), (cross_ref, cross_v)))]
-    stores = [pltpu.make_async_copy(src, dst, load_sem.at[len(mats) + THREE + i]) for i, (src, dst) in enumerate(((dx_v, dx_out), (denc_v, denc_out)))]
 
     def input_grads():
         for copy in loads:
@@ -264,9 +263,7 @@
             return ZERO
 
         lax.fori_loop(ZERO, dx_v.shape[ZERO] // step, decoder, ZERO)
-        stores[ZERO].start()
         lax.fori_loop(ZERO, denc_v.shape[ZERO] // step, encoder, ZERO)
-        stores[ONE].start()
 
     meet_neighbours(scatter.place)
     scatter.begin()
@@ -282,8 +279,6 @@
         scatter.relay(phase)
         scatter.settle(phase)
     scatter.end()
-    for copy in stores:
-        copy.wait()
 
 
 def as_torus(rows):
@@ -298,10 +293,10 @@
     dx_shape, denc_shape = d_self.shape[ONE:], d_cross.shape[ONE:]
     return pl.pallas_call(
         functools.partial(rs_kernel, scale, mats),
-        in_specs=[anywhere] * 6, out_specs=[anywhere] * 4,
+        in_specs=[anywhere] * 6, out_specs=[anywhere] * TWO + [pl.BlockSpec(memory_space=pltpu.VMEM)] * TWO,
         out_shape=[jax.ShapeDtypeStruct((h, src.shape[4]), F32) for h, src in zip(heights, sources)] + [jax.ShapeDtypeStruct(dx_shape, BF16), jax.ShapeDtypeStruct(denc_shape, BF16)],
         scratch_shapes=[pltpu.VMEM((len(mats), d_model, d_model), BF16), pltpu.VMEM(d_res.shape, F32), pltpu.VMEM(d_self.shape, BF16), pltpu.VMEM(d_cross.shape, BF16),
-                        pltpu.VMEM(dx_shape, BF16), pltpu.VMEM(denc_shape, BF16), pltpu.SemaphoreType.DMA((len(mats) + 5,))] + Scatter.scratch_shapes(heights),
+                        pltpu.SemaphoreType.DMA((len(mats) + THREE,))] + Scatter.scratch_shapes(heights),
         compiler_params=pltpu.CompilerParams(collective_id=ONE, has_side_effects=True, vmem_limit_bytes=VMEM_BYTES),
         cost_estimate=pl.CostEstimate(flops=10 ** 9, bytes_accessed=8 * d_model * g_attn.shape[ZERO], transcendentals=ZERO),
         name='scatter_grads',
@@ -525,6 +520,8 @@
                 first, _, far = self.ring(colour, direction)
                 first.wait_recv()
                 far.start()
+
+    def share_near(self):
         for colour in range(COLOURS):
             for direction in range(TWO):
                 self.ring(colour, direction)[ONE].wait_recv()
@@ -736,7 +733,7 @@
 
     turn = sample * pl.num_programs(ONE) + group
     if guest is not None:
-        for where, steps in ((ZERO, (lambda: meet_neighbours(guest.place), guest.begin)), (THREE, (guest.pass_on,)), (5, (guest.complete,))):
+        for where, steps in ((ZERO, (lambda: meet_neighbours(guest.place), guest.begin)), (TWO, (guest.pass_on,)), (THREE, (guest.share_near,)), (4, (guest.complete,))):
             @pl.when(turn == where)
             def _():
                 for step in steps:

time: 302 us -> 305 us (level)
  no operation moved by 1% of the time
where the time goes in v2:
time: 305 us
  Pallas kernels  291 us (95%)
  local copies, waits for them, and re-layouts  9.97 us (3%)
    pallas_call x2, Pallas kernels, attn_backward(): pl.pallas_call(body, grid=(n_batch, n_groups), in_specs=in_specs, out_spe...  94.7 us
    pallas_call x1, Pallas kernels, scatter_grads(): pl.pallas_call(functools.partial(rs_kernel, scale, mats), in_specs=[anywh...  57.1 us
    pallas_call x2, Pallas kernels, attn_forward(): pl.pallas_call(body, grid=(n_batch, n_groups), in_specs=in_specs, out_spe...  50.2 us
    pallas_call x1, Pallas kernels, ffn_both(): pl.pallas_call(functools.partial(ffn_kernel, n_blocks), grid=(n_steps,),...  44.5 us
    pallas_call x1, Pallas kernels, gather_params(): pl.pallas_call(ag_kernel, in_specs=[vmem] * THREE, out_specs=[pl.BlockSpe...  44.5 us

profile of v2, /device:TPU:1, one launch (start us, length us, event | category | flops | bytes accessed | tf_op | source)
XLA Modules:
  0.0 304.8 jit_solution(14373835711764323724)
XLA Ops:
  0.6 0.0 copy-start.7
  0.6 1.3 bitcast_convert_fusion.vec_ref
  1.9 44.5 %gather_params.1 = (bf16[4,4,4,96,768]{4,3,2,1,0:T(8,128)(2,1)}, bf16[3,4,4,16,768]{4,3,2,1,0:T(8,128)(2,1)}, f32[4,4,4,16,128]{4,3,2,1,0:T(8,128)}) custom-call(bf16[96,768]{1,0:T(8,128)(2,1)} %attn_ref.1, bf16[96,768]{1,0:T(8,128)(2,1)} %ffn_ref.1, f32[16,128]{1,0:T(8,128)} %bitcast_convert_fusion.vec_ref), custom_call_target="tpu_custom_call" | custom-call | flops 1000000000 | bytes 18874368 | tf_op jit(solution)/shard_map/gather_params/pallas_call | solution.py:452
  46.5 1.0 slice.69
  47.4 0.1 slice.54
  47.6 0.0 copy-done.7
  47.6 0.7 slice_select_fusion.bias_ref.rows_ref.refs_7_.refs_8_
  48.3 20.7 %attn_fwd.2 = (bf16[1024,768]{1,0:T(8,128)(2,1)}, bf16[1024,768]{1,0:T(8,128)(2,1)}, bf16[1024,768]{1,0:T(8,128)(2,1)}, bf16[1024,768]{1,0:T(8,128)(2,1)}, f32[2...) custom-call(s32[2]{0:T(128)} %refs_0_.5, ...), custom_call_target="tpu_custom_call" | custom-call | flops 11274289152 | bytes 15728640 | tf_op jit(solution)/shard_map/attn_fwd/pallas_call | solution.py:804
  69.0 29.5 %attn_fwd.3 = (bf16[1024,768]{1,0:T(8,128)(2,1)}, bf16[1536,768]{1,0:T(8,128)(2,1)}, bf16[1536,768]{1,0:T(8,128)(2,1)}, bf16[1024,768]{1,0:T(8,128)(2,1)}, f32[2...) custom-call(s32[2]{0:T(128)} %refs_0_.4, ...), custom_call_target="tpu_custom_call" | custom-call | flops 15703474176 | bytes 15728640 | tf_op jit(solution)/shard_map/attn_fwd/pallas_call | solution.py:804
  98.5 0.1 reshape.80
  98.6 0.6 slice.72
  99.2 44.5 %ffn_both.1 = (bf16[1024,768]{1,0:T(8,128)(2,1)}, f32[6144,768]{1,0:T(8,128)}, f32[1024,768]{1,0:T(8,128)}, f32[8,768]{1,0:T(8,128)}, f32[1,3072]{1,0:T(1,128)}) custom-call(bf16[1024,768]{1,0:T(8,128)(2,1)} %get-tuple-element.48.h_ref, bf16[1024,768]{1,0:T(8,128)(2,1)} %bitcast.49, bf16[6144,768]{1,0:T(8,128)(2,1)} %bitcast.54, bf16[6144,768]{1,0:T(8,128)(2,1)} %bitcast.55, ...), custom_call_target="tpu_custom_call" | custom-call | flops 28991029248 | bytes 23592960 | tf_op jit(solution)/shard_map/ffn_both/pallas_call | solution.py:1086
  143.8 66.5 %attn_bwd.2 = (bf16[2,1536,768]{2,1,0:T(8,128)(2,1)}, f32[1024,768]{1,0:T(8,128)}, f32[2,8,768]{2,1,0:T(8,128)}, f32[2,8,768]{2,1,0:T(8,128)}, f32[6144,768]{1,0:T(8,128)}, /*index=5*/f32[96,768]{1,0:T(8,128)}) custom-call(s32[2]{0:T(128)} %refs_0_.4, f32[1024,768]{1,0:T(8,128)} %get-tuple-element.53.refs_1_, bf16[6144,768]{1,0:T(8,128)(2,1)} %bitcast.32, ...), custom_call_target="tpu_custom_call" | custom-call | flops 30198988800 | bytes 15728640 | tf_op jit(solution)/shard_map/attn_bwd/pallas_call | solution.py:1017
  210.3 0.0 copy-start.4
  210.3 0.0 copy-start.3
  210.3 0.0 copy-start.5
  210.3 0.0 copy-start.6
  210.3 28.2 %attn_bwd.3 = (bf16[3,1024,768]{2,1,0:T(8,128)(2,1)}, f32[2,8,768]{2,1,0:T(8,128)}, f32[2,8,768]{2,1,0:T(8,128)}, f32[6144,768]{1,0:T(8,128)}) custom-call(s32[2]{0:T(128)} %refs_0_.5, f32[1024,768]{1,0:T(8,128)} %get-tuple-element.62.refs_1_.dres_ref, bf16[6144,768]{1,0:T(8,128)(2,1)} %bitcast.34, ...), custom_call_target="tpu_custom_call", output_to_operand_aliasing={{3}: (11, {})} | custom-call | flops 20937965568 | bytes 15728640 | tf_op jit(solution)/shard_map/attn_bwd/pallas_call | solution.py:1017
  238.6 0.8 reduce_sum.27
  239.4 0.0 copy-done.4
  239.5 0.0 copy-done.3
  239.6 0.1 slice_reduce_fusion.3
  239.8 0.0 copy-done.6
  239.8 0.2 reshape.87
  240.0 0.8 pad.15
  240.8 57.1 %scatter_grads.1 = (f32[96,768]{1,0:T(8,128)}, f32[8,256]{1,0:T(8,128)}, bf16[1024,768]{1,0:T(8,128)(2,1)}, bf16[1536,768]{1,0:T(8,128)(2,1)}) custom-call(f32[4,4,4,96,768]{4,3,2,1,0:T(8,128)} %bitcast.23, f32[4,4,4,8,256]{4,3,2,1,0:T(8,128)} %bitcast.38, bf16[6144,768]{1,0:T(8,128)(2,1)} %bitcast.36, f32[1024,768]{1,0:T(8,128)} %get-tuple-element.62.refs_1_.dres_ref, ...), custom_call_target="tpu_custom_call" | custom-call | flops 1000000000 | bytes 37748736 | tf_op jit(solution)/shard_map/scatter_grads/pallas_call | solution.py:294
  297.9 1.4 slice.68
  299.3 2.7 copy.35
  302.0 0.0 copy-done
  302.0 1.4 copy.36
  303.4 0.7 copy.37
  304.1 0.7 copy.38
  (27 shorter events, 0.2 us)
Async XLA Ops:
  0.6 46.9 %copy-start.7 = (pred[16]{0:T(512)(128)(4,1)S(1)}, pred[16]{0:T(512)(128)(4,1)}, u32[]{:S(2)}) copy-start(pred[16]{0:T(512)(128)(4,1)} %constant.6.clone.1) | copy-start | bytes 52
  210.3 29.1 %copy-start.4 = (f32[2,8,768]{2,1,0:T(8,128)S(1)}, f32[2,8,768]{2,1,0:T(8,128)}, u32[]{:S(2)}) copy-start(f32[2,8,768]{2,1,0:T(8,128)} %get-tuple-element.71) | copy-start | bytes 147460
  210.3 29.2 %copy-start.3 = (f32[2,8,768]{2,1,0:T(8,128)S(1)}, f32[2,8,768]{2,1,0:T(8,128)}, u32[]{:S(2)}) copy-start(f32[2,8,768]{2,1,0:T(8,128)} %get-tuple-element.72) | copy-start | bytes 147460
  210.3 29.3 %copy-start.5 = (f32[8,768]{1,0:T(8,128)S(1)}, f32[8,768]{1,0:T(8,128)}, u32[]{:S(2)}) copy-start(f32[8,768]{1,0:T(8,128)} %get-tuple-element.73) | copy-start | bytes 73732
  210.3 29.4 %copy-start.6 = (f32[1,3072]{1,0:T(1,128)S(1)}, f32[1,3072]{1,0:T(1,128)}, u32[]{:S(2)}) copy-start(f32[1,3072]{1,0:T(1,128)} %get-tuple-element.74) | copy-start | bytes 36868
  297.9 4.1 %copy-start = (bf16[1536,768]{1,0:T(8,128)(2,1)S(1)}, bf16[1536,768]{1,0:T(8,128)(2,1)}, u32[]{:S(2)}) copy-start(bf16[1536,768]{1,0:T(8,128)(2,1)} %get-tuple-element.78) | copy-start | bytes 7077892
  302.0 1.4 copy-start.2
  302.0 2.1 copy-start.1

commit v3 on v1

--- a/solution.py
+++ b/solution.py
@@ -838,10 +838,9 @@
     d_o = dot_nt(dres_ref[ALL].astype(BF16), wo_ref[ALL]).astype(BF16)
 
     def keep(found, first, width):
-        here = pl.ds(first, width)
         cols = pl.ds(pl.multiple_of(group * GROUP + first, PAIR), width)
         for i, (full, rows, value) in enumerate(zip((d_all, dk_all, dv_all), (q_rows, k_rows, k_rows), found)):
-            sums_ref[ZERO, i:i + ONE, here] = col_sum(value)
+            sums_ref[i:i + ONE, cols] = col_sum(value) + jnp.where(sample == ZERO, 0.0, sums_ref[i:i + ONE, cols])
             full[rows, cols] = value.astype(BF16)
 
     if causal:
@@ -877,9 +876,8 @@
             normed = normed_ref[ALL]
             d_resid = norm_rows_bwd(d_h, normed, inv_ref[ALL], rows_ref[gain_row:gain_row + ONE, :])
             dres_out[ALL] = d_resid
-            tail_ref[ZERO, ZERO:ONE, :] = col_sum(d_resid)
-            tail_ref[ZERO, ONE:TWO, :] = col_sum(d_h * normed)
-            tail_ref[ZERO, TWO:THREE, :] = col_sum(d_h)
+            for i, value in enumerate((d_resid, d_h * normed, d_h)):
+                tail_ref[i:i + ONE, :] = col_sum(value) + jnp.where(sample == ZERO, 0.0, tail_ref[i:i + ONE, :])
 
     @pl.when(turn == pl.num_programs(ZERO) * pl.num_programs(ONE) - ONE)
     def _():
@@ -970,7 +968,8 @@
     in_specs = [pl.BlockSpec(memory_space=pltpu.SMEM), tok(n_q), row(mats[THREE]), anywhere, q_blk, k_blk, k_blk,
                 pl.BlockSpec((ONE, ONE, n_heads_g // TWO, TWO, n_q), lambda b, g: (b, g, ZERO, ZERO, ZERO)), pl.BlockSpec(bias_rows.shape, lambda b, g: (ZERO, ZERO))]
     args = [lens, dres, attn_full, attn_full, q, k, v, lse, bias_rows]
-    tail_shape = jax.ShapeDtypeStruct((n_batch, 8, d_model), F32)
+    tail_shape = jax.ShapeDtypeStruct((8, d_model), F32)
+    whole = pl.BlockSpec((8, d_model), lambda b, g: (ZERO, ZERO))
     out_shape = [jax.ShapeDtypeStruct((THREE,) + q.shape if causal else (TWO,) + k.shape, BF16)]
     out_specs = [anywhere]
     if not causal:
@@ -983,7 +982,7 @@
     args += list(lhs_list)
     in_specs += [anywhere] * len(lhs_list)
     out_shape += [tail_shape, tail_shape, jax.ShapeDtypeStruct(attn_full.shape, F32)]
-    out_specs += [pl.BlockSpec((ONE, 8, GROUP), lambda b, g: (b, ZERO, g)), pl.BlockSpec((ONE, 8, d_model), lambda b, g: (b, ZERO, ZERO)), anywhere]
+    out_specs += [whole, whole, anywhere]
     held = lambda count, n: pltpu.VMEM((count, n_batch * n, d_model), BF16)
     own = [held(4, n_q), held(TWO, n_q)] if causal else [held(TWO, n_q), held(TWO, n_k), held(ONE, n_q), pltpu.VMEM((n_batch * n_k, d_model), BF16)]
     own += [] if causal else [pltpu.VMEM((n_q, GROUP), BF16)]
@@ -1100,7 +1099,7 @@
     )(h2, dy, ffn_full, ffn_full, bias_rows, up_bias, normed2, inv2)
 
 
-CROSS_PLAN = {ONE: (ZERO,), TWO: (ONE,), THREE: (TWO,), 4: (THREE,), 5: (('relay', ZERO),), 9: (('settle', ZERO),), 10: (('relay', ONE),), 'late': (('settle', ONE),), 12: (('relay', TWO),), 13: (('settle', TWO),), 14: ('end',)}
+CROSS_PLAN = {ONE: (ZERO,), THREE: (ONE, TWO), 5: (('relay', ZERO),), 6: (THREE,), 9: (('settle', ZERO),), 11: (('relay', ONE),), 'late': (), 12: (('settle', ONE),), 13: (('relay', TWO),), 14: (('settle', TWO), 'end')}
 
 
 def solution(mesh):
@@ -1128,8 +1127,7 @@
         y, g_ffn, d_res2, ffn_tail, up_sum = ffn_both(h2, dy, ffn_full, bias_rows, up_bias, normed2, inv2)
         d_cross, d_res1, sums2, tail2, grads, ffn_out = attn_backward(d_res2, q2, k2, v2, lse2, src_lens, attn_full, bias_rows, (4, 5, 6, 7), False, (h1, enc, o2), g_ffn, scale, 9, normed1, inv1)
         d_self, sums1, _, grads = attn_backward(d_res1, q1, k1, v1, lse1, tgt_lens, attn_full, bias_rows, (ZERO, ONE, TWO, THREE), True, (x, o1), grads=grads)
-        s1, s2, t2 = jnp.sum(sums1, axis=ZERO), jnp.sum(sums2, axis=ZERO), jnp.sum(tail2, axis=ZERO)
-        g_vec = jnp.concatenate([s1[ZERO:THREE].reshape(-ONE), t2[ZERO], s2[ZERO:THREE].reshape(-ONE), ffn_tail[ZERO], ffn_tail[ONE], t2[ONE], t2[TWO], ffn_tail[TWO], ffn_tail[THREE], ffn_tail[4], ffn_tail[5], up_sum[ZERO]])
+        g_vec = jnp.concatenate([sums1[ZERO:THREE].reshape(-ONE), tail2[ZERO], sums2[ZERO:THREE].reshape(-ONE), ffn_tail[ZERO], ffn_tail[ONE], tail2[ONE], tail2[TWO], ffn_tail[TWO], ffn_tail[THREE], ffn_tail[4], ffn_tail[5], up_sum[ZERO]])
         g_rows = jnp.pad(g_vec.reshape(n_fsdp, ONE, n_vec), ((ZERO, ZERO), (ZERO, 7), (ZERO, TWO * LANES - n_vec))).reshape(n_fsdp * 8, -ONE)
         attn_out, vec_out, d_x, d_enc = scatter_grads(grads, g_rows, scale, attn_full, (ZERO, ONE, TWO, 5, 6), d_res1, d_self, d_cross)
         return y.reshape(dec_in.shape), d_x.reshape(dec_in.shape), d_enc.reshape(enc_out.shape), attn_out, ffn_out, vec_out[ZERO, :n_vec]

time: 302 us -> 302 us (level)
  no operation moved by 1% of the time
where the time goes in v3:
time: 302 us; the launch traced here: 301 us
  Pallas kernels  287 us (95%)
  local copies, waits for them, and re-layouts  11.6 us (4%)
    pallas_call x2, Pallas kernels, attn_backward(): pl.pallas_call(body, grid=(n_batch, n_groups), in_specs=in_specs, out_spe...  91.3 us
    pallas_call x1, Pallas kernels, scatter_grads(): pl.pallas_call(functools.partial(rs_kernel, scale, mats), in_specs=[anywh...  55.9 us
    pallas_call x2, Pallas kernels, attn_forward(): pl.pallas_call(body, grid=(n_batch, n_groups), in_specs=in_specs, out_spe...  50.2 us
    pallas_call x1, Pallas kernels, ffn_both(): pl.pallas_call(functools.partial(ffn_kernel, n_blocks), grid=(n_steps,),...  44.5 us
    pallas_call x1, Pallas kernels, gather_params(): pl.pallas_call(ag_kernel, in_specs=[vmem] * THREE, out_specs=[pl.BlockSpe...  44.5 us

profile of v3, /device:TPU:1, one launch (start us, length us, event | category | flops | bytes accessed | tf_op | source)
XLA Modules:
  0.0 300.9 jit_solution(15901431498483969178)
XLA Ops:
  0.6 0.0 copy-start.6
  0.6 1.3 bitcast_convert_fusion.vec_ref
  1.9 44.5 %gather_params.1 = (bf16[4,4,4,96,768]{4,3,2,1,0:T(8,128)(2,1)}, bf16[3,4,4,16,768]{4,3,2,1,0:T(8,128)(2,1)}, f32[4,4,4,16,128]{4,3,2,1,0:T(8,128)}) custom-call(bf16[96,768]{1,0:T(8,128)(2,1)} %attn_ref.1, bf16[96,768]{1,0:T(8,128)(2,1)} %ffn_ref.1, f32[16,128]{1,0:T(8,128)} %bitcast_convert_fusion.vec_ref), custom_call_target="tpu_custom_call" | custom-call | flops 1000000000 | bytes 18874368 | tf_op jit(solution)/shard_map/gather_params/pallas_call | solution.py:457
  46.5 1.0 slice.69
  47.4 0.1 slice.54
  47.6 0.0 copy-done.6
  47.6 0.7 slice_select_fusion.bias_ref.rows_ref.refs_7_.refs_8_
  48.3 20.7 %attn_fwd.2 = (bf16[1024,768]{1,0:T(8,128)(2,1)}, bf16[1024,768]{1,0:T(8,128)(2,1)}, bf16[1024,768]{1,0:T(8,128)(2,1)}, bf16[1024,768]{1,0:T(8,128)(2,1)}, f32[2...) custom-call(s32[2]{0:T(128)} %refs_0_.5, ...), custom_call_target="tpu_custom_call" | custom-call | flops 11274289152 | bytes 15728640 | tf_op jit(solution)/shard_map/attn_fwd/pallas_call | solution.py:807
  69.0 29.5 %attn_fwd.3 = (bf16[1024,768]{1,0:T(8,128)(2,1)}, bf16[1536,768]{1,0:T(8,128)(2,1)}, bf16[1536,768]{1,0:T(8,128)(2,1)}, bf16[1024,768]{1,0:T(8,128)(2,1)}, f32[2...) custom-call(s32[2]{0:T(128)} %refs_0_.4, ...), custom_call_target="tpu_custom_call" | custom-call | flops 15703474176 | bytes 15728640 | tf_op jit(solution)/shard_map/attn_fwd/pallas_call | solution.py:807
  98.5 0.1 reshape.80
  98.6 0.6 slice.72
  99.2 44.5 %ffn_both.1 = (bf16[1024,768]{1,0:T(8,128)(2,1)}, f32[6144,768]{1,0:T(8,128)}, f32[1024,768]{1,0:T(8,128)}, f32[8,768]{1,0:T(8,128)}, f32[1,3072]{1,0:T(1,128)}) custom-call(bf16[1024,768]{1,0:T(8,128)(2,1)} %get-tuple-element.48.h_ref, bf16[1024,768]{1,0:T(8,128)(2,1)} %bitcast.49, bf16[6144,768]{1,0:T(8,128)(2,1)} %bitcast.54, bf16[6144,768]{1,0:T(8,128)(2,1)} %bitcast.55, ...), custom_call_target="tpu_custom_call" | custom-call | flops 28991029248 | bytes 23592960 | tf_op jit(solution)/shard_map/ffn_both/pallas_call | solution.py:1088
  143.8 63.2 %attn_bwd.2 = (bf16[2,1536,768]{2,1,0:T(8,128)(2,1)}, f32[1024,768]{1,0:T(8,128)}, f32[8,768]{1,0:T(8,128)}, f32[8,768]{1,0:T(8,128)}, f32[6144,768]{1,0:T(8,128)}, /*index=5*/f32[96,768]{1,0:T(8,128)}) custom-call(s32[2]{0:T(128)} %refs_0_.4, f32[1024,768]{1,0:T(8,128)} %get-tuple-element.53.refs_1_, bf16[6144,768]{1,0:T(8,128)(2,1)} %bitcast.32, ...), custom_call_target="tpu_custom_call" | custom-call | flops 30198988800 | bytes 15728640 | tf_op jit(solution)/shard_map/attn_bwd/pallas_call | solution.py:1019
  206.9 0.0 copy-start.5
  207.0 0.0 copy-start.3
  207.0 0.0 copy-start.4
  207.0 28.1 %attn_bwd.3 = (bf16[3,1024,768]{2,1,0:T(8,128)(2,1)}, f32[8,768]{1,0:T(8,128)}, f32[8,768]{1,0:T(8,128)}, f32[6144,768]{1,0:T(8,128)}) custom-call(s32[2]{0:T(128)} %refs_0_.5, f32[1024,768]{1,0:T(8,128)} %get-tuple-element.62.refs_1_.dres_ref, bf16[6144,768]{1,0:T(8,128)(2,1)} %bitcast.34, ...), custom_call_target="tpu_custom_call", output_to_operand_aliasing={{3}: (11, {})} | custom-call | flops 20937965568 | bytes 15728640 | tf_op jit(solution)/shard_map/attn_bwd/pallas_call | solution.py:1019
  235.1 0.7 slice.57
  235.9 0.9 slice_reduce_fusion.4
  236.8 0.0 copy-done.5
  236.9 0.0 copy-done.3
  236.9 0.1 slice_reduce_fusion
  237.0 0.0 copy-done.4
  237.1 0.2 reshape.87
  237.3 0.8 pad.15
  238.1 55.9 %scatter_grads.1 = (f32[96,768]{1,0:T(8,128)}, f32[8,256]{1,0:T(8,128)}, bf16[1024,768]{1,0:T(8,128)(2,1)}, bf16[1536,768]{1,0:T(8,128)(2,1)}) custom-call(f32[4,4,4,96,768]{4,3,2,1,0:T(8,128)} %bitcast.23, f32[4,4,4,8,256]{4,3,2,1,0:T(8,128)} %bitcast.38, bf16[6144,768]{1,0:T(8,128)(2,1)} %bitcast.36, f32[1024,768]{1,0:T(8,128)} %get-tuple-element.62.refs_1_.dres_ref, ...), custom_call_target="tpu_custom_call" | custom-call | flops 1000000000 | bytes 37748736 | tf_op jit(solution)/shard_map/scatter_grads/pallas_call | solution.py:299
  294.0 0.0 copy-start
  294.0 1.4 slice.68
  295.4 2.7 copy.35
  298.1 1.4 copy.36
  299.5 0.7 copy.37
  300.2 0.7 copy.38
  (22 shorter events, 0.1 us)
Async XLA Ops:
  0.6 46.9 %copy-start.6 = (pred[16]{0:T(512)(128)(4,1)S(1)}, pred[16]{0:T(512)(128)(4,1)}, u32[]{:S(2)}) copy-start(pred[16]{0:T(512)(128)(4,1)} %constant.5.clone.1) | copy-start | bytes 52
  206.9 29.9 %copy-start.5 = (f32[8,768]{1,0:T(8,128)S(1)}, f32[8,768]{1,0:T(8,128)}, u32[]{:S(2)}) copy-start(f32[8,768]{1,0:T(8,128)} %get-tuple-element.72) | copy-start | bytes 73732
  207.0 29.9 %copy-start.3 = (f32[8,768]{1,0:T(8,128)S(1)}, f32[8,768]{1,0:T(8,128)}, u32[]{:S(2)}) copy-start(f32[8,768]{1,0:T(8,128)} %get-tuple-element.73) | copy-start | bytes 73732
  207.0 30.1 %copy-start.4 = (f32[1,3072]{1,0:T(1,128)S(1)}, f32[1,3072]{1,0:T(1,128)}, u32[]{:S(2)}) copy-start(f32[1,3072]{1,0:T(1,128)} %get-tuple-element.74) | copy-start | bytes 36868
  294.0 4.1 %copy-start = (bf16[1536,768]{1,0:T(8,128)(2,1)S(1)}, bf16[1536,768]{1,0:T(8,128)(2,1)}, u32[]{:S(2)}) copy-start(bf16[1536,768]{1,0:T(8,128)(2,1)} %get-tuple-element.78) | copy-start | bytes 7077892
  298.1 1.4 copy-start.2
  298.1 2.1 copy-start.1

commit v4 on v1

--- a/solution.py
+++ b/solution.py
@@ -911,6 +911,10 @@
                 return ZERO
 
             def square_k(i, _):
+                @pl.when(i == ONE)
+                def _():
+                    guest(TWO, 14)
+
                 store(i, mats[ONE]).wait()
                 grad_v[i] = dot_tn(lhs_k[ALL], rhs_k[i])
                 store(i, mats[ONE] + i).start()
@@ -920,7 +924,7 @@
             guest(TWO, 13)
             lhs_fetch(ONE).wait()
             lax.fori_loop(ZERO, TWO, square_k, ZERO)
-            guest(TWO, 14)
+            guest(TWO, 15)
         for buf in range(TWO):
             store(buf, mats[ZERO]).wait()
         hand_on.wait()
@@ -1100,7 +1104,7 @@
     )(h2, dy, ffn_full, ffn_full, bias_rows, up_bias, normed2, inv2)
 
 
-CROSS_PLAN = {ONE: (ZERO,), TWO: (ONE,), THREE: (TWO,), 4: (THREE,), 5: (('relay', ZERO),), 9: (('settle', ZERO),), 10: (('relay', ONE),), 'late': (('settle', ONE),), 12: (('relay', TWO),), 13: (('settle', TWO),), 14: ('end',)}
+CROSS_PLAN = {ONE: (ZERO,), THREE: (ONE, TWO), 5: (('relay', ZERO),), 6: (THREE,), 9: (('settle', ZERO),), 11: (('relay', ONE),), 'late': (), 12: (('settle', ONE),), 13: (('relay', TWO),), 14: (('settle', TWO),), 15: ('end',)}
 
 
 def solution(mesh):

time: 302 us -> 300 us (level)
  no operation moved by 1% of the time
where the time goes in v4:
time: 300 us
  Pallas kernels  286 us (95%)
  local copies, waits for them, and re-layouts  9.97 us (3%)
    pallas_call x2, Pallas kernels, attn_backward(): pl.pallas_call(body, grid=(n_batch, n_groups), in_specs=in_specs, out_spe...  91.9 us
    pallas_call x1, Pallas kernels, scatter_grads(): pl.pallas_call(functools.partial(rs_kernel, scale, mats), in_specs=[anywh...  54.9 us
    pallas_call x2, Pallas kernels, attn_forward(): pl.pallas_call(body, grid=(n_batch, n_groups), in_specs=in_specs, out_spe...  50.2 us
    pallas_call x1, Pallas kernels, ffn_both(): pl.pallas_call(functools.partial(ffn_kernel, n_blocks), grid=(n_steps,),...  44.5 us
    pallas_call x1, Pallas kernels, gather_params(): pl.pallas_call(ag_kernel, in_specs=[vmem] * THREE, out_specs=[pl.BlockSpe...  44.5 us

profile of v4, /device:TPU:1, one launch (start us, length us, event | category | flops | bytes accessed | tf_op | source)
XLA Modules:
  0.0 299.7 jit_solution(8022430368925739998)
XLA Ops:
  0.6 0.0 copy-start.7
  0.6 1.3 bitcast_convert_fusion.vec_ref
  1.9 44.5 %gather_params.1 = (bf16[4,4,4,96,768]{4,3,2,1,0:T(8,128)(2,1)}, bf16[3,4,4,16,768]{4,3,2,1,0:T(8,128)(2,1)}, f32[4,4,4,16,128]{4,3,2,1,0:T(8,128)}) custom-call(bf16[96,768]{1,0:T(8,128)(2,1)} %attn_ref.1, bf16[96,768]{1,0:T(8,128)(2,1)} %ffn_ref.1, f32[16,128]{1,0:T(8,128)} %bitcast_convert_fusion.vec_ref), custom_call_target="tpu_custom_call" | custom-call | flops 1000000000 | bytes 18874368 | tf_op jit(solution)/shard_map/gather_params/pallas_call | solution.py:457
  46.5 1.0 slice.69
  47.4 0.1 slice.54
  47.6 0.0 copy-done.7
  47.6 0.7 slice_select_fusion.bias_ref.rows_ref.refs_7_.refs_8_
  48.3 20.7 %attn_fwd.2 = (bf16[1024,768]{1,0:T(8,128)(2,1)}, bf16[1024,768]{1,0:T(8,128)(2,1)}, bf16[1024,768]{1,0:T(8,128)(2,1)}, bf16[1024,768]{1,0:T(8,128)(2,1)}, f32[2...) custom-call(s32[2]{0:T(128)} %refs_0_.5, ...), custom_call_target="tpu_custom_call" | custom-call | flops 11274289152 | bytes 15728640 | tf_op jit(solution)/shard_map/attn_fwd/pallas_call | solution.py:807
  69.0 29.5 %attn_fwd.3 = (bf16[1024,768]{1,0:T(8,128)(2,1)}, bf16[1536,768]{1,0:T(8,128)(2,1)}, bf16[1536,768]{1,0:T(8,128)(2,1)}, bf16[1024,768]{1,0:T(8,128)(2,1)}, f32[2...) custom-call(s32[2]{0:T(128)} %refs_0_.4, ...), custom_call_target="tpu_custom_call" | custom-call | flops 15703474176 | bytes 15728640 | tf_op jit(solution)/shard_map/attn_fwd/pallas_call | solution.py:807
  98.5 0.1 reshape.80
  98.6 0.6 slice.72
  99.2 44.5 %ffn_both.1 = (bf16[1024,768]{1,0:T(8,128)(2,1)}, f32[6144,768]{1,0:T(8,128)}, f32[1024,768]{1,0:T(8,128)}, f32[8,768]{1,0:T(8,128)}, f32[1,3072]{1,0:T(1,128)}) custom-call(bf16[1024,768]{1,0:T(8,128)(2,1)} %get-tuple-element.48.h_ref, bf16[1024,768]{1,0:T(8,128)(2,1)} %bitcast.49, bf16[6144,768]{1,0:T(8,128)(2,1)} %bitcast.54, bf16[6144,768]{1,0:T(8,128)(2,1)} %bitcast.55, ...), custom_call_target="tpu_custom_call" | custom-call | flops 28991029248 | bytes 23592960 | tf_op jit(solution)/shard_map/ffn_both/pallas_call | solution.py:1093
  143.8 63.6 %attn_bwd.2 = (bf16[2,1536,768]{2,1,0:T(8,128)(2,1)}, f32[1024,768]{1,0:T(8,128)}, f32[2,8,768]{2,1,0:T(8,128)}, f32[2,8,768]{2,1,0:T(8,128)}, f32[6144,768]{1,0:T(8,128)}, /*index=5*/f32[96,768]{1,0:T(8,128)}) custom-call(s32[2]{0:T(128)} %refs_0_.4, f32[1024,768]{1,0:T(8,128)} %get-tuple-element.53.refs_1_, bf16[6144,768]{1,0:T(8,128)(2,1)} %bitcast.32, ...), custom_call_target="tpu_custom_call" | custom-call | flops 30198988800 | bytes 15728640 | tf_op jit(solution)/shard_map/attn_bwd/pallas_call | solution.py:1024
  207.4 0.0 copy-start.4
  207.4 0.0 copy-start.3
  207.4 0.0 copy-start.5
  207.4 0.0 copy-start.6
  207.4 28.2 %attn_bwd.3 = (bf16[3,1024,768]{2,1,0:T(8,128)(2,1)}, f32[2,8,768]{2,1,0:T(8,128)}, f32[2,8,768]{2,1,0:T(8,128)}, f32[6144,768]{1,0:T(8,128)}) custom-call(s32[2]{0:T(128)} %refs_0_.5, f32[1024,768]{1,0:T(8,128)} %get-tuple-element.62.refs_1_.dres_ref, bf16[6144,768]{1,0:T(8,128)(2,1)} %bitcast.34, ...), custom_call_target="tpu_custom_call", output_to_operand_aliasing={{3}: (11, {})} | custom-call | flops 20937965568 | bytes 15728640 | tf_op jit(solution)/shard_map/attn_bwd/pallas_call | solution.py:1024
  235.7 0.8 reduce_sum.27
  236.5 0.0 copy-done.4
  236.6 0.0 copy-done.3
  236.7 0.1 slice_reduce_fusion.3
  236.9 0.2 reshape.87
  237.1 0.8 pad.15
  237.9 54.9 %scatter_grads.1 = (f32[96,768]{1,0:T(8,128)}, f32[8,256]{1,0:T(8,128)}, bf16[1024,768]{1,0:T(8,128)(2,1)}, bf16[1536,768]{1,0:T(8,128)(2,1)}) custom-call(f32[4,4,4,96,768]{4,3,2,1,0:T(8,128)} %bitcast.23, f32[4,4,4,8,256]{4,3,2,1,0:T(8,128)} %bitcast.38, bf16[6144,768]{1,0:T(8,128)(2,1)} %bitcast.36, f32[1024,768]{1,0:T(8,128)} %get-tuple-element.62.refs_1_.dres_ref, ...), custom_call_target="tpu_custom_call" | custom-call | flops 1000000000 | bytes 37748736 | tf_op jit(solution)/shard_map/scatter_grads/pallas_call | solution.py:299
  292.8 1.4 slice.68
  294.2 2.7 copy.35
  296.9 1.4 copy.36
  298.3 0.0 copy-done.2
  298.3 0.7 copy.37
  299.0 0.0 copy-done.1
  299.0 0.7 copy.38
  (27 shorter events, 0.2 us)
Async XLA Ops:
  0.6 46.9 %copy-start.7 = (pred[16]{0:T(512)(128)(4,1)S(1)}, pred[16]{0:T(512)(128)(4,1)}, u32[]{:S(2)}) copy-start(pred[16]{0:T(512)(128)(4,1)} %constant.6.clone.1) | copy-start | bytes 52
  207.4 29.1 %copy-start.4 = (f32[2,8,768]{2,1,0:T(8,128)S(1)}, f32[2,8,768]{2,1,0:T(8,128)}, u32[]{:S(2)}) copy-start(f32[2,8,768]{2,1,0:T(8,128)} %get-tuple-element.71) | copy-start | bytes 147460
  207.4 29.2 %copy-start.3 = (f32[2,8,768]{2,1,0:T(8,128)S(1)}, f32[2,8,768]{2,1,0:T(8,128)}, u32[]{:S(2)}) copy-start(f32[2,8,768]{2,1,0:T(8,128)} %get-tuple-element.72) | copy-start | bytes 147460
  207.4 29.3 %copy-start.5 = (f32[8,768]{1,0:T(8,128)S(1)}, f32[8,768]{1,0:T(8,128)}, u32[]{:S(2)}) copy-start(f32[8,768]{1,0:T(8,128)} %get-tuple-element.73) | copy-start | bytes 73732
  207.4 29.4 %copy-start.6 = (f32[1,3072]{1,0:T(1,128)S(1)}, f32[1,3072]{1,0:T(1,128)}, u32[]{:S(2)}) copy-start(f32[1,3072]{1,0:T(1,128)} %get-tuple-element.74) | copy-start | bytes 36868
  292.8 4.1 %copy-start = (bf16[1536,768]{1,0:T(8,128)(2,1)S(1)}, bf16[1536,768]{1,0:T(8,128)(2,1)}, u32[]{:S(2)}) copy-start(bf16[1536,768]{1,0:T(8,128)(2,1)} %get-tuple-element.78) | copy-start | bytes 7077892
  296.9 1.4 copy-start.2
  296.9 2.1 copy-start.1

commit v5 on v1

--- a/solution.py
+++ b/solution.py
@@ -1100,7 +1100,7 @@
     )(h2, dy, ffn_full, ffn_full, bias_rows, up_bias, normed2, inv2)
 
 
-CROSS_PLAN = {ONE: (ZERO,), TWO: (ONE,), THREE: (TWO,), 4: (THREE,), 5: (('relay', ZERO),), 9: (('settle', ZERO),), 10: (('relay', ONE),), 'late': (('settle', ONE),), 12: (('relay', TWO),), 13: (('settle', TWO),), 14: ('end',)}
+CROSS_PLAN = {ONE: (ZERO,), THREE: (ONE, TWO), 5: (('relay', ZERO),), 6: (THREE,), 9: (('settle', ZERO),), 11: (('relay', ONE),), 'late': (), 12: (('settle', ONE),), 13: (('relay', TWO),), 14: (('settle', TWO), 'end')}
 
 
 def solution(mesh):

time: 302 us -> 301 us (level)
  no operation moved by 1% of the time
where the time goes in v5:
time: 301 us; the launch traced here: 300 us
  Pallas kernels  287 us (95%)
  local copies, waits for them, and re-layouts  9.97 us (3%)
    pallas_call x2, Pallas kernels, attn_backward(): pl.pallas_call(body, grid=(n_batch, n_groups), in_specs=in_specs, out_spe...  91.5 us
    pallas_call x1, Pallas kernels, scatter_grads(): pl.pallas_call(functools.partial(rs_kernel, scale, mats), in_specs=[anywh...  56 us
    pallas_call x2, Pallas kernels, attn_forward(): pl.pallas_call(body, grid=(n_batch, n_groups), in_specs=in_specs, out_spe...  50.2 us
    pallas_call x1, Pallas kernels, ffn_both(): pl.pallas_call(functools.partial(ffn_kernel, n_blocks), grid=(n_steps,),...  44.5 us
    pallas_call x1, Pallas kernels, gather_params(): pl.pallas_call(ag_kernel, in_specs=[vmem] * THREE, out_specs=[pl.BlockSpe...  44.5 us

profile of v5, /device:TPU:1, one launch (start us, length us, event | category | flops | bytes accessed | tf_op | source)
XLA Modules:
  0.0 300.5 jit_solution(5774005883939958810)
XLA Ops:
  0.6 0.0 copy-start.7
  0.6 1.3 bitcast_convert_fusion.vec_ref
  1.9 44.5 %gather_params.1 = (bf16[4,4,4,96,768]{4,3,2,1,0:T(8,128)(2,1)}, bf16[3,4,4,16,768]{4,3,2,1,0:T(8,128)(2,1)}, f32[4,4,4,16,128]{4,3,2,1,0:T(8,128)}) custom-call(bf16[96,768]{1,0:T(8,128)(2,1)} %attn_ref.1, bf16[96,768]{1,0:T(8,128)(2,1)} %ffn_ref.1, f32[16,128]{1,0:T(8,128)} %bitcast_convert_fusion.vec_ref), custom_call_target="tpu_custom_call" | custom-call | flops 1000000000 | bytes 18874368 | tf_op jit(solution)/shard_map/gather_params/pallas_call | solution.py:457
  46.5 1.0 slice.69
  47.4 0.1 slice.54
  47.6 0.0 copy-done.7
  47.6 0.7 slice_select_fusion.bias_ref.rows_ref.refs_7_.refs_8_
  48.3 20.7 %attn_fwd.2 = (bf16[1024,768]{1,0:T(8,128)(2,1)}, bf16[1024,768]{1,0:T(8,128)(2,1)}, bf16[1024,768]{1,0:T(8,128)(2,1)}, bf16[1024,768]{1,0:T(8,128)(2,1)}, f32[2...) custom-call(s32[2]{0:T(128)} %refs_0_.5, ...), custom_call_target="tpu_custom_call" | custom-call | flops 11274289152 | bytes 15728640 | tf_op jit(solution)/shard_map/attn_fwd/pallas_call | solution.py:807
  69.0 29.5 %attn_fwd.3 = (bf16[1024,768]{1,0:T(8,128)(2,1)}, bf16[1536,768]{1,0:T(8,128)(2,1)}, bf16[1536,768]{1,0:T(8,128)(2,1)}, bf16[1024,768]{1,0:T(8,128)(2,1)}, f32[2...) custom-call(s32[2]{0:T(128)} %refs_0_.4, ...), custom_call_target="tpu_custom_call" | custom-call | flops 15703474176 | bytes 15728640 | tf_op jit(solution)/shard_map/attn_fwd/pallas_call | solution.py:807
  98.5 0.1 reshape.80
  98.6 0.6 slice.72
  99.2 44.5 %ffn_both.1 = (bf16[1024,768]{1,0:T(8,128)(2,1)}, f32[6144,768]{1,0:T(8,128)}, f32[1024,768]{1,0:T(8,128)}, f32[8,768]{1,0:T(8,128)}, f32[1,3072]{1,0:T(1,128)}) custom-call(bf16[1024,768]{1,0:T(8,128)(2,1)} %get-tuple-element.48.h_ref, bf16[1024,768]{1,0:T(8,128)(2,1)} %bitcast.49, bf16[6144,768]{1,0:T(8,128)(2,1)} %bitcast.54, bf16[6144,768]{1,0:T(8,128)(2,1)} %bitcast.55, ...), custom_call_target="tpu_custom_call" | custom-call | flops 28991029248 | bytes 23592960 | tf_op jit(solution)/shard_map/ffn_both/pallas_call | solution.py:1089
  143.8 63.2 %attn_bwd.2 = (bf16[2,1536,768]{2,1,0:T(8,128)(2,1)}, f32[1024,768]{1,0:T(8,128)}, f32[2,8,768]{2,1,0:T(8,128)}, f32[2,8,768]{2,1,0:T(8,128)}, f32[6144,768]{1,0:T(8,128)}, /*index=5*/f32[96,768]{1,0:T(8,128)}) custom-call(s32[2]{0:T(128)} %refs_0_.4, f32[1024,768]{1,0:T(8,128)} %get-tuple-element.53.refs_1_, bf16[6144,768]{1,0:T(8,128)(2,1)} %bitcast.32, ...), custom_call_target="tpu_custom_call" | custom-call | flops 30198988800 | bytes 15728640 | tf_op jit(solution)/shard_map/attn_bwd/pallas_call | solution.py:1020
  207.0 0.0 copy-start.4
  207.0 0.0 copy-start.3
  207.0 0.0 copy-start.5
  207.0 0.0 copy-start.6
  207.1 28.2 %attn_bwd.3 = (bf16[3,1024,768]{2,1,0:T(8,128)(2,1)}, f32[2,8,768]{2,1,0:T(8,128)}, f32[2,8,768]{2,1,0:T(8,128)}, f32[6144,768]{1,0:T(8,128)}) custom-call(s32[2]{0:T(128)} %refs_0_.5, f32[1024,768]{1,0:T(8,128)} %get-tuple-element.62.refs_1_.dres_ref, bf16[6144,768]{1,0:T(8,128)(2,1)} %bitcast.34, ...), custom_call_target="tpu_custom_call", output_to_operand_aliasing={{3}: (11, {})} | custom-call | flops 20937965568 | bytes 15728640 | tf_op jit(solution)/shard_map/attn_bwd/pallas_call | solution.py:1020
  235.3 0.8 reduce_sum.27
  236.1 0.0 copy-done.4
  236.2 0.0 copy-done.3
  236.3 0.0 copy-done.5
  236.3 0.1 slice_reduce_fusion.3
  236.5 0.0 copy-done.6
  236.5 0.2 reshape.87
  236.7 0.8 pad.15
  237.5 56.0 %scatter_grads.1 = (f32[96,768]{1,0:T(8,128)}, f32[8,256]{1,0:T(8,128)}, bf16[1024,768]{1,0:T(8,128)(2,1)}, bf16[1536,768]{1,0:T(8,128)(2,1)}) custom-call(f32[4,4,4,96,768]{4,3,2,1,0:T(8,128)} %bitcast.23, f32[4,4,4,8,256]{4,3,2,1,0:T(8,128)} %bitcast.38, bf16[6144,768]{1,0:T(8,128)(2,1)} %bitcast.36, f32[1024,768]{1,0:T(8,128)} %get-tuple-element.62.refs_1_.dres_ref, ...), custom_call_target="tpu_custom_call" | custom-call | flops 1000000000 | bytes 37748736 | tf_op jit(solution)/shard_map/scatter_grads/pallas_call | solution.py:299
  293.5 1.4 slice.68
  295.0 2.7 copy.35
  297.6 1.4 copy.36
  299.0 0.7 copy.37
  299.7 0.7 copy.38
  (27 shorter events, 0.2 us)
Async XLA Ops:
  0.6 46.9 %copy-start.7 = (pred[16]{0:T(512)(128)(4,1)S(1)}, pred[16]{0:T(512)(128)(4,1)}, u32[]{:S(2)}) copy-start(pred[16]{0:T(512)(128)(4,1)} %constant.6.clone.1) | copy-start | bytes 52
  207.0 29.1 %copy-start.4 = (f32[2,8,768]{2,1,0:T(8,128)S(1)}, f32[2,8,768]{2,1,0:T(8,128)}, u32[]{:S(2)}) copy-start(f32[2,8,768]{2,1,0:T(8,128)} %get-tuple-element.71) | copy-start | bytes 147460
  207.0 29.2 %copy-start.3 = (f32[2,8,768]{2,1,0:T(8,128)S(1)}, f32[2,8,768]{2,1,0:T(8,128)}, u32[]{:S(2)}) copy-start(f32[2,8,768]{2,1,0:T(8,128)} %get-tuple-element.72) | copy-start | bytes 147460
  207.0 29.3 %copy-start.5 = (f32[8,768]{1,0:T(8,128)S(1)}, f32[8,768]{1,0:T(8,128)}, u32[]{:S(2)}) copy-start(f32[8,768]{1,0:T(8,128)} %get-tuple-element.73) | copy-start | bytes 73732
  207.0 29.4 %copy-start.6 = (f32[1,3072]{1,0:T(1,128)S(1)}, f32[1,3072]{1,0:T(1,128)}, u32[]{:S(2)}) copy-start(f32[1,3072]{1,0:T(1,128)} %get-tuple-element.74) | copy-start | bytes 36868
  293.5 4.1 %copy-start = (bf16[1536,768]{1,0:T(8,128)(2,1)S(1)}, bf16[1536,768]{1,0:T(8,128)(2,1)}, u32[]{:S(2)}) copy-start(bf16[1536,768]{1,0:T(8,128)(2,1)} %get-tuple-element.78) | copy-start | bytes 7077892
  297.6 1.4 copy-start.2
  297.6 2.1 copy-start.1

commit v6 on v4

--- a/solution.py
+++ b/solution.py
@@ -270,10 +270,11 @@
 
     meet_neighbours(scatter.place)
     scatter.begin()
-    for copy in loads:
-        copy.start()
     for turn in range(THREE):
         scatter.absorb(turn)
+        if turn == ONE:
+            for copy in loads:
+                copy.start()
     scatter.relay(ZERO)
     scatter.absorb(THREE)
     input_grads()

time: 300 us -> 300 us (level)
  no operation moved by 1% of the time
where the time goes in v6:
time: 300 us; the launch traced here: 299 us
  Pallas kernels  285 us (95%)
  local copies, waits for them, and re-layouts  9.97 us (3%)
    pallas_call x2, Pallas kernels, attn_backward(): pl.pallas_call(body, grid=(n_batch, n_groups), in_specs=in_specs, out_spe...  91.9 us
    pallas_call x1, Pallas kernels, scatter_grads(): pl.pallas_call(functools.partial(rs_kernel, scale, mats), in_specs=[anywh...  54.2 us
    pallas_call x2, Pallas kernels, attn_forward(): pl.pallas_call(body, grid=(n_batch, n_groups), in_specs=in_specs, out_spe...  50.2 us
    pallas_call x1, Pallas kernels, ffn_both(): pl.pallas_call(functools.partial(ffn_kernel, n_blocks), grid=(n_steps,),...  44.5 us
    pallas_call x1, Pallas kernels, gather_params(): pl.pallas_call(ag_kernel, in_specs=[vmem] * THREE, out_specs=[pl.BlockSpe...  44.5 us

profile of v6, /device:TPU:1, one launch (start us, length us, event | category | flops | bytes accessed | tf_op | source)
XLA Modules:
  0.0 299.0 jit_solution(11579117310502898612)
XLA Ops:
  0.6 0.0 copy-start.7
  0.6 1.3 bitcast_convert_fusion.vec_ref
  1.9 44.5 %gather_params.1 = (bf16[4,4,4,96,768]{4,3,2,1,0:T(8,128)(2,1)}, bf16[3,4,4,16,768]{4,3,2,1,0:T(8,128)(2,1)}, f32[4,4,4,16,128]{4,3,2,1,0:T(8,128)}) custom-call(bf16[96,768]{1,0:T(8,128)(2,1)} %attn_ref.1, bf16[96,768]{1,0:T(8,128)(2,1)} %ffn_ref.1, f32[16,128]{1,0:T(8,128)} %bitcast_convert_fusion.vec_ref), custom_call_target="tpu_custom_call" | custom-call | flops 1000000000 | bytes 18874368 | tf_op jit(solution)/shard_map/gather_params/pallas_call | solution.py:458
  46.5 1.0 slice.69
  47.4 0.1 slice.54
  47.6 0.0 copy-done.7
  47.6 0.7 slice_select_fusion.bias_ref.rows_ref.refs_7_.refs_8_
  48.3 20.7 %attn_fwd.2 = (bf16[1024,768]{1,0:T(8,128)(2,1)}, bf16[1024,768]{1,0:T(8,128)(2,1)}, bf16[1024,768]{1,0:T(8,128)(2,1)}, bf16[1024,768]{1,0:T(8,128)(2,1)}, f32[2...) custom-call(s32[2]{0:T(128)} %refs_0_.5, ...), custom_call_target="tpu_custom_call" | custom-call | flops 11274289152 | bytes 15728640 | tf_op jit(solution)/shard_map/attn_fwd/pallas_call | solution.py:808
  69.0 29.5 %attn_fwd.3 = (bf16[1024,768]{1,0:T(8,128)(2,1)}, bf16[1536,768]{1,0:T(8,128)(2,1)}, bf16[1536,768]{1,0:T(8,128)(2,1)}, bf16[1024,768]{1,0:T(8,128)(2,1)}, f32[2...) custom-call(s32[2]{0:T(128)} %refs_0_.4, ...), custom_call_target="tpu_custom_call" | custom-call | flops 15703474176 | bytes 15728640 | tf_op jit(solution)/shard_map/attn_fwd/pallas_call | solution.py:808
  98.5 0.1 reshape.80
  98.6 0.6 slice.72
  99.2 44.5 %ffn_both.1 = (bf16[1024,768]{1,0:T(8,128)(2,1)}, f32[6144,768]{1,0:T(8,128)}, f32[1024,768]{1,0:T(8,128)}, f32[8,768]{1,0:T(8,128)}, f32[1,3072]{1,0:T(1,128)}) custom-call(bf16[1024,768]{1,0:T(8,128)(2,1)} %get-tuple-element.48.h_ref, bf16[1024,768]{1,0:T(8,128)(2,1)} %bitcast.49, bf16[6144,768]{1,0:T(8,128)(2,1)} %bitcast.54, bf16[6144,768]{1,0:T(8,128)(2,1)} %bitcast.55, ...), custom_call_target="tpu_custom_call" | custom-call | flops 28991029248 | bytes 23592960 | tf_op jit(solution)/shard_map/ffn_both/pallas_call | solution.py:1094
  143.8 63.6 %attn_bwd.2 = (bf16[2,1536,768]{2,1,0:T(8,128)(2,1)}, f32[1024,768]{1,0:T(8,128)}, f32[2,8,768]{2,1,0:T(8,128)}, f32[2,8,768]{2,1,0:T(8,128)}, f32[6144,768]{1,0:T(8,128)}, /*index=5*/f32[96,768]{1,0:T(8,128)}) custom-call(s32[2]{0:T(128)} %refs_0_.4, f32[1024,768]{1,0:T(8,128)} %get-tuple-element.53.refs_1_, bf16[6144,768]{1,0:T(8,128)(2,1)} %bitcast.32, ...), custom_call_target="tpu_custom_call" | custom-call | flops 30198988800 | bytes 15728640 | tf_op jit(solution)/shard_map/attn_bwd/pallas_call | solution.py:1025
  207.4 0.0 copy-start.4
  207.4 0.0 copy-start.3
  207.4 0.0 copy-start.5
  207.4 0.0 copy-start.6
  207.4 28.2 %attn_bwd.3 = (bf16[3,1024,768]{2,1,0:T(8,128)(2,1)}, f32[2,8,768]{2,1,0:T(8,128)}, f32[2,8,768]{2,1,0:T(8,128)}, f32[6144,768]{1,0:T(8,128)}) custom-call(s32[2]{0:T(128)} %refs_0_.5, f32[1024,768]{1,0:T(8,128)} %get-tuple-element.62.refs_1_.dres_ref, bf16[6144,768]{1,0:T(8,128)(2,1)} %bitcast.34, ...), custom_call_target="tpu_custom_call", output_to_operand_aliasing={{3}: (11, {})} | custom-call | flops 20937965568 | bytes 15728640 | tf_op jit(solution)/shard_map/attn_bwd/pallas_call | solution.py:1025
  235.7 0.8 reduce_sum.27
  236.5 0.0 copy-done.4
  236.6 0.0 copy-done.3
  236.7 0.0 copy-done.5
  236.7 0.1 slice_reduce_fusion.3
  236.9 0.2 reshape.87
  237.1 0.8 pad.15
  237.9 54.2 %scatter_grads.1 = (f32[96,768]{1,0:T(8,128)}, f32[8,256]{1,0:T(8,128)}, bf16[1024,768]{1,0:T(8,128)(2,1)}, bf16[1536,768]{1,0:T(8,128)(2,1)}) custom-call(f32[4,4,4,96,768]{4,3,2,1,0:T(8,128)} %bitcast.23, f32[4,4,4,8,256]{4,3,2,1,0:T(8,128)} %bitcast.38, bf16[6144,768]{1,0:T(8,128)(2,1)} %bitcast.36, f32[1024,768]{1,0:T(8,128)} %get-tuple-element.62.refs_1_.dres_ref, ...), custom_call_target="tpu_custom_call" | custom-call | flops 1000000000 | bytes 37748736 | tf_op jit(solution)/shard_map/scatter_grads/pallas_call | solution.py:300
  292.1 1.4 slice.68
  293.5 2.7 copy.35
  296.2 1.4 copy.36
  297.6 0.7 copy.37
  298.3 0.0 copy-done.1
  298.3 0.7 copy.38
  (27 shorter events, 0.2 us)
Async XLA Ops:
  0.6 46.9 %copy-start.7 = (pred[16]{0:T(512)(128)(4,1)S(1)}, pred[16]{0:T(512)(128)(4,1)}, u32[]{:S(2)}) copy-start(pred[16]{0:T(512)(128)(4,1)} %constant.6.clone.1) | copy-start | bytes 52
  207.4 29.1 %copy-start.4 = (f32[2,8,768]{2,1,0:T(8,128)S(1)}, f32[2,8,768]{2,1,0:T(8,128)}, u32[]{:S(2)}) copy-start(f32[2,8,768]{2,1,0:T(8,128)} %get-tuple-element.71) | copy-start | bytes 147460
  207.4 29.2 %copy-start.3 = (f32[2,8,768]{2,1,0:T(8,128)S(1)}, f32[2,8,768]{2,1,0:T(8,128)}, u32[]{:S(2)}) copy-start(f32[2,8,768]{2,1,0:T(8,128)} %get-tuple-element.72) | copy-start | bytes 147460
  207.4 29.3 %copy-start.5 = (f32[8,768]{1,0:T(8,128)S(1)}, f32[8,768]{1,0:T(8,128)}, u32[]{:S(2)}) copy-start(f32[8,768]{1,0:T(8,128)} %get-tuple-element.73) | copy-start | bytes 73732
  207.4 29.4 %copy-start.6 = (f32[1,3072]{1,0:T(1,128)S(1)}, f32[1,3072]{1,0:T(1,128)}, u32[]{:S(2)}) copy-start(f32[1,3072]{1,0:T(1,128)} %get-tuple-element.74) | copy-start | bytes 36868
  292.1 4.1 %copy-start = (bf16[1536,768]{1,0:T(8,128)(2,1)S(1)}, bf16[1536,768]{1,0:T(8,128)(2,1)}, u32[]{:S(2)}) copy-start(bf16[1536,768]{1,0:T(8,128)(2,1)} %get-tuple-element.78) | copy-start | bytes 7077892
  296.2 1.4 copy-start.2
  296.2 2.1 copy-start.1
